TPU v7x, 128 devices: a whole 4x4x4 slice. The times are simulated.
128 devices in a mesh: ctx: 16 (over z, x_lo, core), tp: 8 (over x_hi, y).
Axes of the slice: x: 4 (x_hi: 2, x_lo: 2; x = x_hi * 2 + x_lo), y: 4, z: 4, core: 2. Of those that a mesh axis runs over, the one named last changes fastest.
Arguments:
- tokens: bfloat16 [2, 4096, 8192], P(None, 'ctx', 'tp'), may hold values from -14 to 14
- norm_gain: float32 [8192], replicated, may hold values from 0.5 to 1.5
- span_order: int32 [2, 32], replicated, may hold values from 0 to 31, each once within a row
- w_query: bfloat16 [8192, 4096], P('ctx', 'tp'), may hold values from -0.10122281 to 0.10122281
- w_key: bfloat16 [8192, 1024], P('ctx', 'tp'), may hold values from -0.10122281 to 0.10122281
- value_weight: bfloat16 [8192, 1024], P('ctx', 'tp'), may hold values from -0.0625 to 0.0625
- w_out: bfloat16 [4096, 8192], P('tp', 'ctx'), may hold values from -0.75 to 0.75
Outputs:
- mixed: bfloat16 [2, 4096, 8192], P(None, 'ctx', 'tp')
Inputs may be any that keep to these rules, and one draw needn't show every extreme that they name: Each row of span_order names every one of the 2 * 16 blocks of positions once; stored block b of a sequence holds positions span_order[b] * 128 onwards, in order.
All inputs are finite; a program needn't handle non-finite values.
Results may differ from a plain program's by a relative error of at most 0.014.
Values may be sent and summed in bfloat16 or wider, within the bound.
A program may use at most 128 MiB of HBM per device.

v0:
```python
import math

import jax
import jax.numpy as jnp
from jax import lax
from jax.sharding import PartitionSpec as P

HEAD_DIM = 128


theta_base = 500000.0
norm_eps = 1e-05
masked_score = -1e30


def in_one_piece(arrays, axis, dim, along):
    ends, at = ([], 0)
    for a in arrays[:-1]:
        at += a.shape[along]
        ends.append(at)
    both = jnp.concatenate(arrays, axis=along)
    return tuple(jnp.split(lax.all_gather(both, axis, axis=dim, tiled=True), ends, axis=along))


def normalize(flat_rows, norm_gain):
    wide = flat_rows.astype(jnp.float32)
    factor = lax.rsqrt(jnp.mean(wide * wide, axis=-1, keepdims=True) + norm_eps)
    return (wide * factor * norm_gain).astype(jnp.bfloat16)


def positions_of(span_order, first, count, block_rows):
    stored = first + jnp.arange(count, dtype=jnp.int32)
    which = stored // block_rows
    slots = jnp.arange(span_order.shape[1], dtype=jnp.int32)
    picked = jnp.sum(
        jnp.where(slots[None, None, :] == which[None, :, None], span_order[:, None, :], 0), axis=2
    )
    return picked * block_rows + stored % block_rows


def apply_rotation(value_rows, token_position, head_size):
    half = head_size // 2
    freqs = jnp.exp(-(2.0 * jnp.arange(half, dtype=jnp.float32) / head_size) * math.log(theta_base))
    angle = token_position.astype(jnp.float32)[..., None] * freqs
    cosine = jnp.cos(angle)[:, :, None, :]
    sine = jnp.sin(angle)[:, :, None, :]
    front = value_rows[..., :half]
    back = value_rows[..., half:]
    return jnp.concatenate([front * cosine - back * sine, back * cosine + front * sine], axis=-1)


def per_device(tokens, norm_gain, span_order, w_query, w_key, value_weight, w_out):
    sequence_batch, rows_dev, _ = tokens.shape
    head_size = HEAD_DIM
    query_heads = w_query.shape[1] // head_size
    key_heads = w_key.shape[1] // head_size
    group_width = query_heads // key_heads
    block_rows = rows_dev // 2
    total_rows = sequence_batch * rows_dev
    factor = 1.0 / math.sqrt(head_size)
    rank = lax.axis_index("ctx")
    whole = lax.all_gather(tokens, "tp", axis=2, tiled=True)
    normed = normalize(whole.reshape(total_rows, whole.shape[2]), norm_gain)
    query_pos = positions_of(span_order, rank * rows_dev, rows_dev, block_rows)
    latest = jnp.max(query_pos, axis=1)
    stat_shape = (sequence_batch, key_heads, group_width, rows_dev)
    initial = (
        jnp.full(stat_shape, masked_score, jnp.float32),
        jnp.zeros(stat_shape, jnp.float32),
        jnp.zeros(stat_shape + (head_size,), jnp.float32),
    )
    pieces = in_one_piece((w_query, w_key, value_weight), "ctx", 0, 1)
    query_flat, flattened_key, flattened_value = tuple(
        (jnp.dot(normed, piece, preferred_element_type=jnp.float32) for piece in pieces)
    )
    turned = apply_rotation(
        query_flat.reshape(sequence_batch, rows_dev, query_heads, head_size), query_pos, head_size
    ).astype(jnp.bfloat16)
    query = turned.reshape(sequence_batch, rows_dev, key_heads, group_width, head_size).transpose(
        0, 2, 3, 1, 4
    )
    turned = apply_rotation(
        flattened_key.reshape(sequence_batch, rows_dev, key_heads, head_size), query_pos, head_size
    ).astype(jnp.bfloat16)
    own_values = flattened_value.reshape(sequence_batch, rows_dev, key_heads, head_size).astype(
        jnp.bfloat16
    )
    key_piece, value_piece = in_one_piece((turned, own_values), "ctx", 1, 0)
    count = key_piece.shape[1]
    step_rows = 512

    def one_block(index, state):
        first = index * step_rows
        key_block = lax.dynamic_slice_in_dim(key_piece, first, step_rows, 1)
        value_block = lax.dynamic_slice_in_dim(value_piece, first, step_rows, 1)
        key_pos = positions_of(span_order, first, step_rows, block_rows)

        def update(current):
            peak, total, summed = current
            scores = (
                jnp.einsum(
                    "shgqd,skhd->shgqk", query, key_block, preferred_element_type=jnp.float32
                )
                * factor
            )
            allowed = key_pos[:, None, None, None, :] <= query_pos[:, None, None, :, None]
            scores = jnp.where(allowed, scores, masked_score)
            new_peak = jnp.maximum(peak, jnp.max(scores, axis=-1))
            weights = jnp.where(allowed, jnp.exp(scores - new_peak[..., None]), 0.0)
            shrink = jnp.exp(peak - new_peak)
            total = total * shrink + jnp.sum(weights, axis=-1)
            summed = summed * shrink[..., None] + jnp.einsum(
                "shgqk,skhd->shgqd",
                weights.astype(jnp.bfloat16),
                value_block,
                preferred_element_type=jnp.float32,
            )
            return (new_peak, total, summed)

        return lax.cond(
            jnp.all(jnp.min(key_pos, axis=1) > latest), lambda kept: kept, update, state
        )

    peak, total, summed = lax.fori_loop(0, count // step_rows, one_block, initial)
    attended = (summed / total[..., None]).astype(jnp.bfloat16)
    attended = attended.transpose(0, 3, 1, 2, 4).reshape(total_rows, query_heads * head_size)
    terms = jnp.dot(
        attended,
        lax.all_gather(w_out, "ctx", axis=1, tiled=True),
        preferred_element_type=jnp.float32,
    )
    mixed = lax.psum_scatter(terms.astype(jnp.bfloat16), "tp", scatter_dimension=1, tiled=True)
    return mixed.reshape(sequence_batch, rows_dev, mixed.shape[1])


def solution(mesh):
    placed = (
        P(None, "ctx", "tp"),
        P(),
        P(),
        P("ctx", "tp"),
        P("ctx", "tp"),
        P("ctx", "tp"),
        P("tp", "ctx"),
    )
    return jax.shard_map(
        per_device, mesh=mesh, in_specs=placed, out_specs=P(None, "ctx", "tp"), check_vma=False
    )
```

profile of v0, /device:TPU:0, one launch (start us, length us, event | category | flops | bytes accessed | tf_op | source)
XLA Modules:
  0.0 453.7 jit_solution(2648720766434171846)
XLA Ops:
  6.5 0.7 all-gather.5.cloned.1.call-update
  7.3 1.3 copy.28
  8.6 1.0 copy.29
  9.6 1.0 copy.30
  10.6 0.9 pad_maximum_fusion
  11.8 106.8 %all-gather.5.cloned.1.call-done = bf16[2,256,8192]{2,1,0:T(8,128)(2,1)} async-done(((bf16[2,256,1024]{2,1,0:T(8,128)(2,1)}), bf16[2,256,8192]{2,1,0:T(8,128)(2,1)}) %all-gather.5.cloned.1.call-update) | async-done | bytes 8388624 | tf_op jit(solution)/shard_map/all_gather | solution.py:62
  118.6 5.1 %fusion.27 = f32[2,256]{1,0:T(2,128)S(1)} fusion(bf16[2,256,8192]{2,1,0:T(8,128)(2,1)} %all-gather.5.cloned.1.call-done), kind=kLoop, calls=%fused_computation.41 | loop fusion | flops 12582400 | bytes 8390656 | tf_op jit(solution)/shard_map/reduce_sum | solution.py:27
  123.7 66.3 %all-gather.7.cloned.1.call-done = bf16[8192,768]{0,1:T(8,128)(2,1)} async-done(((bf16[512,768]{0,1:T(8,128)(2,1)}), bf16[8192,768]{0,1:T(8,128)(2,1)}) %all-gather.7.cloned.1.call-update) | async-done | bytes 12582928 | tf_op jit(solution)/shard_map/all_gather | solution.py:22
  190.0 7.0 %fusion.37 = f32[2,256,1,128]{1,3,0,2:T(8,128)S(1)} fusion(bf16[8192,768]{0,1:T(8,128)(2,1)} %all-gather.7.cloned.1.call-done, bf16[2,256,8192]{2,1,0:T(8,128)(2,1)} %all-gather.5.cloned.1.call-done, f32[8192]{0:T(1024)S(1)} %copy-done.1, f32[2,256]{1,0:T(2,128)S(1)} %add_rsqrt_fusion), kind=kOutput, calls=%fused_computation.51 | convolution fusion | flops 1090519040 | bytes 10782720 | tf_op jit(solution)/shard_map/dot_general | solution.py:74
  197.1 0.6 fusion.56
  197.6 7.0 %fusion.43 = bf16[2,256,1,128]{1,3,0,2:T(8,128)(2,1)S(1)} fusion(bf16[8192,768]{0,1:T(8,128)(2,1)} %all-gather.7.cloned.1.call-done, bf16[2,256,8192]{2,1,0:T(8,128)(2,1)} %all-gather.5.cloned.1.call-done, f32[8192]{0:T(1024)S(1)} %copy-done.1, f32[2,256]{1,0:T(2,128)S(1)} %add_rsqrt_fusion), kind=kOutput, calls=%fused_computation.53 | convolution fusion | flops 1090584576 | bytes 10651648 | tf_op jit(solution)/shard_map/dot_general | solution.py:74
  204.6 0.7 pad_maximum_fusion.1
  205.4 0.5 all-gather.11.cloned.1.call-update
  206.3 0.5 multiply_cosine_fusion
  206.8 7.7 %split.23 = bf16[8192,512]{0,1:T(8,128)(2,1)} slice(bf16[8192,768]{0,1:T(8,128)(2,1)} %all-gather.7.cloned.1.call-done), slice={[0:8192], [0:512]} | slice | bytes 16777216 | tf_op jit(solution)/shard_map/split | solution.py:22
  214.6 9.8 %fusion.30 = f32[2,256,4,128]{1,3,2,0:T(8,128)S(1)} fusion(bf16[4,128,8192,1]{2,1,0,3:T(8,128)(2,1)} %bitcast.90, bf16[2,256,8192]{2,1,0:T(8,128)(2,1)} %all-gather.5.cloned.1.call-done, f32[8192]{0:T(1024)S(1)} %copy-done.1, f32[2,256]{1,0:T(2,128)S(1)} %add_rsqrt_fusion), kind=kOutput, calls=%fused_computation.45 | convolution fusion | flops 4311744512 | bytes 17860608 | tf_op jit(solution)/shard_map/dot_general | solution.py:74
  224.8 26.8 %all-gather.9.cloned.1.call-done = bf16[4,4096,1,128]{1,3,0,2:T(8,128)(2,1)} async-done(((bf16[4,256,1,128]{1,3,0,2:T(8,128)(2,1)}), bf16[4,4096,1,128]{1,3,0,2:T(8,128)(2,1)}) %all-gather.9.cloned.1.call-update) | async-done | bytes 4194320 | tf_op jit(solution)/shard_map/all_gather | solution.py:22
  251.6 3.9 fusion.62
  255.5 4.1 copy.33
  259.6 2.4 copy.35
  262.1 59.5 %while.19 = (s32[]{:T(128)}, f32[2,1,4,256]{3,2,0,1:T(4,128)S(1)}, f32[2,1,4,256]{3,2,0,1:T(4,128)S(1)}, f32[2,1,4,256,128]{4,3,2,0,1:T(8,128)S(1)}, s32[2,32]{1...) while((s32[]{:T(128)}, f32[2,1,4,256]{3,2,0,1:T(4,128)S(1)}, ...), condition=%wide.region_11.12_spmd, body=%wide.region_3.11_spmd.sunk | while | flops 551389184 | bytes 16968260 | solution.py:124
  262.4 0.7 compare_reduce_fusion.2
  263.8 5.7 %conditional.2 = (f32[2,1,4,256]{3,2,0,1:T(4,128)S(1)}, f32[2,1,4,256]{3,2,0,1:T(4,128)S(1)}, f32[2,1,4,256,128]{4,3,2,0,1:T(8,128)S(1)}) conditional(s32[]{:T(128)} %convert_element_type.120, (s32[2,512]{1,0:T(2,128)S(1)}, s32[2,256]{1,0:T(2,128)S(1)}, s32[]{:T(128)}, bf16[2,4096,1,128]{3,1,0,2:T(8,128)(2,1)}, ...), branch_computations={%region_7.9_spmd, %region_10.10_spmd} | conditional | flops 551294976 | bytes 16898114 | solution.py:120
  264.0 1.8 fusion
  265.8 2.6 fusion.9
  268.4 1.0 fusion.2
  269.8 0.7 compare_reduce_fusion.2
  271.2 5.8 %conditional.2 = (f32[2,1,4,256]{3,2,0,1:T(4,128)S(1)}, f32[2,1,4,256]{3,2,0,1:T(4,128)S(1)}, f32[2,1,4,256,128]{4,3,2,0,1:T(8,128)S(1)}) conditional(s32[]{:T(128)} %convert_element_type.120, (s32[2,512]{1,0:T(2,128)S(1)}, s32[2,256]{1,0:T(2,128)S(1)}, s32[]{:T(128)}, bf16[2,4096,1,128]{3,1,0,2:T(8,128)(2,1)}, ...), branch_computations={%region_7.9_spmd, %region_10.10_spmd} | conditional | flops 551294976 | bytes 16898114 | solution.py:120
  271.4 1.8 fusion
  273.2 2.6 fusion.9
  275.9 1.0 fusion.2
  277.2 0.7 compare_reduce_fusion.2
  278.6 5.8 %conditional.2 = (f32[2,1,4,256]{3,2,0,1:T(4,128)S(1)}, f32[2,1,4,256]{3,2,0,1:T(4,128)S(1)}, f32[2,1,4,256,128]{4,3,2,0,1:T(8,128)S(1)}) conditional(s32[]{:T(128)} %convert_element_type.120, (s32[2,512]{1,0:T(2,128)S(1)}, s32[2,256]{1,0:T(2,128)S(1)}, s32[]{:T(128)}, bf16[2,4096,1,128]{3,1,0,2:T(8,128)(2,1)}, ...), branch_computations={%region_7.9_spmd, %region_10.10_spmd} | conditional | flops 551294976 | bytes 16898114 | solution.py:120
  278.9 1.8 fusion
  280.7 2.7 fusion.9
  283.3 1.0 fusion.2
  284.7 0.7 compare_reduce_fusion.2
  286.1 5.8 %conditional.2 = (f32[2,1,4,256]{3,2,0,1:T(4,128)S(1)}, f32[2,1,4,256]{3,2,0,1:T(4,128)S(1)}, f32[2,1,4,256,128]{4,3,2,0,1:T(8,128)S(1)}) conditional(s32[]{:T(128)} %convert_element_type.120, (s32[2,512]{1,0:T(2,128)S(1)}, s32[2,256]{1,0:T(2,128)S(1)}, s32[]{:T(128)}, bf16[2,4096,1,128]{3,1,0,2:T(8,128)(2,1)}, ...), branch_computations={%region_7.9_spmd, %region_10.10_spmd} | conditional | flops 551294976 | bytes 16898114 | solution.py:120
  286.3 1.8 fusion
  288.1 2.6 fusion.9
  290.8 1.0 fusion.2
  292.1 0.7 compare_reduce_fusion.2
  293.5 5.8 %conditional.2 = (f32[2,1,4,256]{3,2,0,1:T(4,128)S(1)}, f32[2,1,4,256]{3,2,0,1:T(4,128)S(1)}, f32[2,1,4,256,128]{4,3,2,0,1:T(8,128)S(1)}) conditional(s32[]{:T(128)} %convert_element_type.120, (s32[2,512]{1,0:T(2,128)S(1)}, s32[2,256]{1,0:T(2,128)S(1)}, s32[]{:T(128)}, bf16[2,4096,1,128]{3,1,0,2:T(8,128)(2,1)}, ...), branch_computations={%region_7.9_spmd, %region_10.10_spmd} | conditional | flops 551294976 | bytes 16898114 | solution.py:120
  293.8 1.8 fusion
  295.6 2.6 fusion.9
  298.2 1.0 fusion.2
  299.6 0.7 compare_reduce_fusion.2
  301.0 5.8 %conditional.2 = (f32[2,1,4,256]{3,2,0,1:T(4,128)S(1)}, f32[2,1,4,256]{3,2,0,1:T(4,128)S(1)}, f32[2,1,4,256,128]{4,3,2,0,1:T(8,128)S(1)}) conditional(s32[]{:T(128)} %convert_element_type.120, (s32[2,512]{1,0:T(2,128)S(1)}, s32[2,256]{1,0:T(2,128)S(1)}, s32[]{:T(128)}, bf16[2,4096,1,128]{3,1,0,2:T(8,128)(2,1)}, ...), branch_computations={%region_7.9_spmd, %region_10.10_spmd} | conditional | flops 551294976 | bytes 16898114 | solution.py:120
  301.2 1.8 fusion
  303.0 2.7 fusion.9
  305.7 1.0 fusion.2
  307.0 0.7 compare_reduce_fusion.2
  308.4 5.8 %conditional.2 = (f32[2,1,4,256]{3,2,0,1:T(4,128)S(1)}, f32[2,1,4,256]{3,2,0,1:T(4,128)S(1)}, f32[2,1,4,256,128]{4,3,2,0,1:T(8,128)S(1)}) conditional(s32[]{:T(128)} %convert_element_type.120, (s32[2,512]{1,0:T(2,128)S(1)}, s32[2,256]{1,0:T(2,128)S(1)}, s32[]{:T(128)}, bf16[2,4096,1,128]{3,1,0,2:T(8,128)(2,1)}, ...), branch_computations={%region_7.9_spmd, %region_10.10_spmd} | conditional | flops 551294976 | bytes 16898114 | solution.py:120
  308.7 1.8 fusion
  310.5 2.6 fusion.9
  313.1 1.0 fusion.2
  314.5 0.7 compare_reduce_fusion.2
  315.9 5.8 %conditional.2 = (f32[2,1,4,256]{3,2,0,1:T(4,128)S(1)}, f32[2,1,4,256]{3,2,0,1:T(4,128)S(1)}, f32[2,1,4,256,128]{4,3,2,0,1:T(8,128)S(1)}) conditional(s32[]{:T(128)} %convert_element_type.120, (s32[2,512]{1,0:T(2,128)S(1)}, s32[2,256]{1,0:T(2,128)S(1)}, s32[]{:T(128)}, bf16[2,4096,1,128]{3,1,0,2:T(8,128)(2,1)}, ...), branch_computations={%region_7.9_spmd, %region_10.10_spmd} | conditional | flops 551294976 | bytes 16898114 | solution.py:120
  316.1 1.8 fusion
  317.9 2.6 fusion.9
  320.5 1.0 fusion.2
  322.0 0.4 copy.36
  322.4 10.1 %convolution_convert_fusion = bf16[512,8192]{1,0:T(8,128)(2,1)} fusion(bf16[512,8192]{1,0:T(8,128)(2,1)} %all-gather.11.cloned.1.call-done, bf16[64,8,4,128]{3,2,1,0:T(4,128)(2,1)S(1)} %bitcast.93), kind=kOutput, calls=%fused_computation.44 | convolution fusion | flops 4299161600 | bytes 17301504 | tf_op jit(solution)/shard_map/dot_general | solution.py:127
  332.6 114.6 %reduce-scatter.2.cloned.1.call-done = bf16[512,1024]{1,0:T(8,128)(2,1)} async-done(((bf16[512,8192]{1,0:T(8,128)(2,1)}), bf16[512,1024]{1,0:T(8,128)(2,1)}) %reduce-scatter.2.cloned.1.call-update) | async-done | bytes 1048592 | tf_op jit(solution)/shard_map/reduce_scatter | solution.py:132
  (91 shorter events, 5.5 us)
Async XLA Ops:
  6.5 5.1 %copy-start = (s32[2,32]{1,0:T(2,128)S(1)}, s32[2,32]{1,0:T(2,128)}, u32[]{:S(2)}) copy-start(s32[2,32]{1,0:T(2,128)} %param.13) | copy-start | bytes 772
  6.5 112.1 %all-gather.5.cloned.1.call-start = ((), (), s32[]{:S(2)}) async-start(), calls=%async_computation.1 | async-start | bytes 9437184 | tf_op jit(solution)/shard_map/all_gather | solution.py:62
  7.3 182.8 %all-gather.7.cloned.1.call-start = ((), (), s32[]{:S(2)}) async-start(), calls=%async_computation.2 | async-start | bytes 13369344 | tf_op jit(solution)/shard_map/all_gather | solution.py:22
  11.5 240.1 %all-gather.9.cloned.1.call-start = ((), (), s32[]{:S(2)}) async-start(), calls=%async_computation.3 | async-start | bytes 4456448 | tf_op jit(solution)/shard_map/all_gather | solution.py:22
  11.8 178.3 %copy-start.1 = (f32[8192]{0:T(1024)S(1)}, f32[8192]{0:T(1024)}, u32[]{:S(2)}) copy-start(f32[8192]{0:T(1024)} %param.12) | copy-start | bytes 98308
  205.4 117.0 %all-gather.11.cloned.1.call-start = ((), (), s32[]{:S(2)}) async-start(), calls=%async_computation.4 | async-start | bytes 8912896 | tf_op jit(solution)/shard_map/all_gather | solution.py:129
  206.0 241.2 %reduce-scatter.2.cloned.1.call-start = ((), (), s32[]{:S(2)}) async-start(), calls=%async_computation.5 | async-start | bytes 9437184 | tf_op jit(solution)/shard_map/reduce_scatter | solution.py:132
Sparse Core Ops, SparseCore 0:
  9.6 108.9 all-gather.4
  120.3 69.7 all-gather.6
  205.5 46.0 all-gather.8
  253.1 52.2 all-gather.10
  332.7 114.4 reduce-scatter.1
where the time goes:
time: 455 us; the launch traced here: 454 us
  waiting for transfers between devices  316 us (69%)
  matrix products  69.2 us (15%)
  other arithmetic  26.5 us (6%)
  local copies, waits for them, and re-layouts  22.2 us (5%)
  between operations  13.3 us (3%)
  loops' own time  6.33 us (1%)
    reduce_scatter x1, waiting for transfers between devices, per_device(): lax.psum_scatter(terms.astype(jnp.bfloat16), 'tp', scatter_dimension=1, t...  115 us
    all_gather x1, waiting for transfers between devices, per_device(): whole = lax.all_gather(tokens, 'tp', axis=2, tiled=True)  107 us
    all_gather x2, waiting for transfers between devices, in_one_piece(): lax.all_gather(both, axis, axis=dim, tiled=True)  93.1 us
    dot_general x3, matrix products, per_device(): jnp.dot(normed, piece, preferred_element_type=jnp.float32)  23.8 us
    dot_general x8, matrix products, update(): jnp.einsum('shgqk,skhd->shgqd', weights.astype(jnp.bfloat16), value_block...  21.2 us
    dot_general x8, matrix products, update(): jnp.einsum('shgqd,skhd->shgqk', query, key_block, preferred_element_type=...  14.2 us
    split x2, local copies, waits for them, and re-layouts, in_one_piece(): jnp.split(lax.all_gather(both, axis, axis=dim, tiled=True), ends, axis=al...  11.6 us
    dot_general x1, matrix products, per_device(): jnp.dot(attended, lax.all_gather(w_out, 'ctx', axis=1, tiled=True), prefe...  10.1 us
  transfers between devices with their start and end apart: 5, of which 4 were waited for; matrix products, arithmetic and copies ran while one was open for 20% of the time, Pallas kernels for 0%

commit v1 on v0

--- a/solution.py
+++ b/solution.py
@@ -3,6 +3,8 @@
 import jax
 import jax.numpy as jnp
 from jax import lax
+from jax.experimental import pallas as pl
+from jax.experimental.pallas import tpu as pltpu
 from jax.sharding import PartitionSpec as P
 
 HEAD_DIM = 128
@@ -20,12 +22,6 @@
         ends.append(at)
     both = jnp.concatenate(arrays, axis=along)
     return tuple(jnp.split(lax.all_gather(both, axis, axis=dim, tiled=True), ends, axis=along))
-
-
-def normalize(flat_rows, norm_gain):
-    wide = flat_rows.astype(jnp.float32)
-    factor = lax.rsqrt(jnp.mean(wide * wide, axis=-1, keepdims=True) + norm_eps)
-    return (wide * factor * norm_gain).astype(jnp.bfloat16)
 
 
 def positions_of(span_order, first, count, block_rows):
@@ -38,15 +34,352 @@
     return picked * block_rows + stored % block_rows
 
 
-def apply_rotation(value_rows, token_position, head_size):
-    half = head_size // 2
-    freqs = jnp.exp(-(2.0 * jnp.arange(half, dtype=jnp.float32) / head_size) * math.log(theta_base))
+def angles(token_position):
+    half = HEAD_DIM // 2
+    freqs = jnp.exp(-(2.0 * jnp.arange(half, dtype=jnp.float32) / HEAD_DIM) * math.log(theta_base))
     angle = token_position.astype(jnp.float32)[..., None] * freqs
-    cosine = jnp.cos(angle)[:, :, None, :]
-    sine = jnp.sin(angle)[:, :, None, :]
-    front = value_rows[..., :half]
-    back = value_rows[..., half:]
-    return jnp.concatenate([front * cosine - back * sine, back * cosine + front * sine], axis=-1)
+    cosine, sine = jnp.cos(angle), jnp.sin(angle)
+    return jnp.concatenate([cosine, cosine], axis=-1), jnp.concatenate([-sine, sine], axis=-1)
+
+
+MESH = pl.DeviceIdType.MESH
+
+
+def neighbours():
+    ctx, tp = lax.axis_index("ctx"), lax.axis_index("tp")
+    z, xl, core = ctx // 4, (ctx // 2) % 2, ctx % 2
+    xh, y = tp // 4, tp % 4
+
+    def at(z_, xl_, core_, xh_, y_):
+        return {"ctx": z_ * 4 + xl_ * 2 + core_, "tp": xh_ * 4 + y_}
+
+    return {
+        "yp": at(z, xl, core, xh, (y + 1) % 4),
+        "ym": at(z, xl, core, xh, (y + 3) % 4),
+        "xh": at(z, xl, core, 1 - xh, y),
+        "zp": at((z + 1) % 4, xl, core, xh, y),
+        "zm": at((z + 3) % 4, xl, core, xh, y),
+        "xl": at(z, 1 - xl, core, xh, y),
+        "co": at(z, xl, 1 - core, xh, y),
+    }
+
+
+class Links:
+    def __init__(self, send, recv):
+        self.send, self.recv, self.count = send, recv, 0
+        self.where = neighbours()
+        self.sent = []
+
+    def greet(self, names):
+        barrier = pltpu.get_barrier_semaphore()
+        for name in names:
+            pl.semaphore_signal(barrier, 1, device_id=self.where[name], device_id_type=MESH)
+        pl.semaphore_wait(barrier, len(names))
+
+    def ticket(self):
+        self.count += 1
+        return self.count - 1
+
+    def copy(self, ticket, src, dst, name):
+        return pltpu.make_async_remote_copy(
+            src, dst, self.send.at[ticket], self.recv.at[ticket],
+            device_id=self.where[name], device_id_type=MESH,
+        )
+
+    def start(self, ticket, src, dst, name):
+        c = self.copy(ticket, src, dst, name)
+        c.start()
+        self.sent.append(c)
+
+    def arrive(self, ticket, here, name="co"):
+        self.copy(ticket, here, here, name).wait_recv()
+
+    def finish(self):
+        for c in self.sent:
+            c.wait_send()
+        self.sent = []
+
+
+def token_flow(links, tokens_buf, source):
+    tp = lax.axis_index("tp")
+    xh, y = tp // 4, tp % 4
+
+    def shard(dx, dy):
+        return (xh if dx == 0 else 1 - xh) * 4 + (y + dy) % 4
+
+    def slot(dx, dy, s, rows=None):
+        ref = tokens_buf.at[shard(dx, dy) * 2 + s]
+        return ref if rows is None else ref.at[pl.ds(rows[0], rows[1])]
+
+    events = []
+    rows = tokens_buf.shape[1]
+    low, high = (0, rows // 2), (rows // 2, rows // 2)
+    T = {}
+    for s in range(2):
+        for k in ("yp", "ym", "xh", "fa", "fb", "pyp", "pym", "x2"):
+            T[k, s] = links.ticket()
+
+    def own(s):
+        links.start(T["xh", s], source.at[s], slot(0, 0, s), "xh")
+        links.start(T["yp", s], source.at[s], slot(0, 0, s), "yp")
+        links.start(T["ym", s], source.at[s], slot(0, 0, s), "ym")
+
+    def forward(s):
+        links.arrive(T["yp", s], slot(0, 3, s), "ym")
+        links.start(T["fa", s], slot(0, 3, s, low), slot(0, 3, s, low), "yp")
+        links.arrive(T["ym", s], slot(0, 1, s), "yp")
+        links.start(T["fb", s], slot(0, 1, s, high), slot(0, 1, s, high), "ym")
+
+    def partner(s):
+        links.arrive(T["xh", s], slot(1, 0, s), "xh")
+        links.start(T["pyp", s], slot(1, 0, s), slot(1, 0, s), "yp")
+        links.start(T["pym", s], slot(1, 0, s), slot(1, 0, s), "ym")
+
+    def across(s):
+        links.arrive(T["fa", s], slot(0, 2, s, low), "ym")
+        links.arrive(T["fb", s], slot(0, 2, s, high), "yp")
+        links.start(T["x2", s], slot(0, 2, s), slot(0, 2, s), "xh")
+
+    def sides(s):
+        links.arrive(T["pyp", s], slot(1, 3, s), "ym")
+        links.arrive(T["pym", s], slot(1, 1, s), "yp")
+
+    def last(s):
+        links.arrive(T["x2", s], slot(1, 2, s), "xh")
+
+    return dict(own=own, forward=forward, partner=partner, across=across, sides=sides, last=last, shard=shard)
+
+
+def squares_flow(links, buf):
+    tp = lax.axis_index("tp")
+    xh, y = tp // 4, tp % 4
+
+    def slot(dx, dy):
+        return buf.at[(xh if dx == 0 else 1 - xh) * 4 + (y + dy) % 4]
+
+    ring = [links.ticket() for _ in range(3)]
+    cross = [links.ticket() for _ in range(4)]
+
+    def own():
+        links.start(ring[0], slot(0, 0), slot(0, 0), "yp")
+        links.start(ring[1], slot(0, 0), slot(0, 0), "ym")
+        links.start(cross[0], slot(0, 0), slot(0, 0), "xh")
+
+    def all_():
+        links.arrive(ring[0], slot(0, 3), "ym")
+        links.start(ring[2], slot(0, 3), slot(0, 3), "yp")
+        links.start(cross[3], slot(0, 3), slot(0, 3), "xh")
+        links.arrive(ring[1], slot(0, 1), "yp")
+        links.start(cross[1], slot(0, 1), slot(0, 1), "xh")
+        links.arrive(ring[2], slot(0, 2), "ym")
+        links.start(cross[2], slot(0, 2), slot(0, 2), "xh")
+        for dy in range(4):
+            links.arrive(cross[dy], slot(1, dy), "xh")
+
+    return {"own": own, "all": all_}
+
+
+def column_flow(links, buf, halves=2):
+    ctx = lax.axis_index("ctx")
+    z, xl, core = ctx // 4, (ctx // 2) % 2, ctx % 2
+    rows = buf.shape[1]
+    half = rows // 2
+
+    def slot(dx, dz, dc=0, part=None):
+        i = ((z + dz) % 4) * 4 + (xl if dx == 0 else 1 - xl) * 2 + (core if dc == 0 else 1 - core)
+        ref = buf.at[i]
+        return ref if part is None else ref.at[pl.ds(part * half, half)]
+
+    T = {}
+    for k in ("zp", "zm", "xl0", "xl1", "fa", "fb", "pzp0", "pzp1", "pzm0", "pzm1", "pfa", "pfb"):
+        T[k] = links.ticket()
+    for dx in range(2):
+        for dz in range(4):
+            T["co", dx, dz] = links.ticket()
+
+    def share(dx, dz):
+        links.start(T["co", dx, dz], slot(dx, dz), slot(dx, dz), "co")
+
+    def own_x(part):
+        links.start(T[f"xl{part}"], slot(0, 0, 0, part), slot(0, 0, 0, part), "xl")
+
+    def own_z():
+        links.start(T["zp"], slot(0, 0), slot(0, 0), "zp")
+        links.start(T["zm"], slot(0, 0), slot(0, 0), "zm")
+        share(0, 0)
+
+    def forward():
+        links.arrive(T["zp"], slot(0, 3), "zm")
+        links.start(T["fa"], slot(0, 3, 0, 0), slot(0, 3, 0, 0), "zp")
+        links.arrive(T["zm"], slot(0, 1), "zp")
+        links.start(T["fb"], slot(0, 1, 0, 1), slot(0, 1, 0, 1), "zm")
+        share(0, 3)
+        share(0, 1)
+
+    def partner(part):
+        links.arrive(T[f"xl{part}"], slot(1, 0, 0, part), "xl")
+        links.start(T[f"pzp{part}"], slot(1, 0, 0, part), slot(1, 0, 0, part), "zp")
+        links.start(T[f"pzm{part}"], slot(1, 0, 0, part), slot(1, 0, 0, part), "zm")
+        if part == 1:
+            share(1, 0)
+
+    def across():
+        links.arrive(T["fa"], slot(0, 2, 0, 0), "zm")
+        links.arrive(T["fb"], slot(0, 2, 0, 1), "zp")
+        share(0, 2)
+
+    def sides():
+        links.arrive(T["pzp0"], slot(1, 3, 0, 0), "zm")
+        links.start(T["pfa"], slot(1, 3, 0, 0), slot(1, 3, 0, 0), "zp")
+        links.arrive(T["pzm0"], slot(1, 1, 0, 0), "zp")
+        links.arrive(T["pzm1"], slot(1, 1, 0, 1), "zp")
+        links.start(T["pfb"], slot(1, 1, 0, 1), slot(1, 1, 0, 1), "zm")
+        links.arrive(T["pzp1"], slot(1, 3, 0, 1), "zm")
+        share(1, 3)
+        share(1, 1)
+
+    def last():
+        links.arrive(T["pfa"], slot(1, 2, 0, 0), "zm")
+        links.arrive(T["pfb"], slot(1, 2, 0, 1), "zp")
+        share(1, 2)
+
+    def shared(pairs):
+        for dx, dz in pairs:
+            links.arrive(T["co", dx, dz], slot(dx, dz, 1), "co")
+
+    everything = [(dx, dz) for dx in range(2) for dz in range(4)]
+    return dict(own_x=own_x, own_z=own_z, forward=forward, partner=partner, across=across, sides=sides,
+                last=last, shared=shared, everything=everything)
+
+
+def project_kernel(tokens, wq, wk, wv, gain, cosine, sine, q_out, kv_out,
+                   tbuf, wbuf, acc, squares, factors, send, recv, local):
+    links = Links(send, recv)
+    ctx, tp = lax.axis_index("ctx"), lax.axis_index("tp")
+    qw, kw = wq.shape[1], wk.shape[1]
+    width = qw + 2 * kw
+    mine = [
+        pltpu.make_async_copy(wq, wbuf.at[ctx, :, pl.ds(0, qw)], local.at[0]),
+        pltpu.make_async_copy(wk, wbuf.at[ctx, :, pl.ds(qw, kw)], local.at[1]),
+        pltpu.make_async_copy(wv, wbuf.at[ctx, :, pl.ds(qw + kw, kw)], local.at[2]),
+        pltpu.make_async_copy(tokens, tbuf.at[pl.ds(tp * 2, 2)], local.at[3]),
+    ]
+    for c in mine:
+        c.start()
+    t = token_flow(links, tbuf, tokens)
+    w = column_flow(links, wbuf)
+    links.greet(("yp", "ym", "xh", "zp", "zm", "xl", "co"))
+    for c in mine[:3]:
+        c.wait()
+    w["own_x"](0)
+    t["own"](0)
+    w["own_z"]()
+    w["own_x"](1)
+    t["own"](1)
+    mine[3].wait()
+    rows = tokens.shape[1]
+    for s in range(2):
+        wide = tbuf[tp * 2 + s].astype(jnp.float32)
+        squares[tp, s] = lax.dot_general(
+            jnp.ones((8, wide.shape[1]), jnp.float32), wide * wide, (((1,), (1,)), ((), ())),
+            precision=lax.Precision.HIGHEST, preferred_element_type=jnp.float32,
+        )
+    acc[...] = jnp.zeros_like(acc)
+    statistics = squares_flow(links, squares)
+    statistics["own"]()
+
+    t["forward"](0)
+    w["forward"]()
+    w["partner"](0)
+    t["partner"](0)
+    t["forward"](1)
+    w["partner"](1)
+    w["across"]()
+    t["across"](0)
+    t["partner"](1)
+    t["across"](1)
+    w["sides"]()
+    t["sides"](0)
+    w["last"]()
+    w["shared"](w["everything"])
+    statistics["all"]()
+    features = 8 * tokens.shape[2]
+    for s in range(2):
+        total = squares[0, s]
+        for i in range(1, 8):
+            total = total + squares[i, s]
+        factor = lax.rsqrt(total[:1] * (1.0 / features) + norm_eps)
+        factors[s] = jnp.transpose(jnp.broadcast_to(factor, (128, rows)))
+
+    def multiply(j, s):
+        dx, dy = j // 4, j % 4
+        shard = (tp // 4 + dx) % 2 * 4 + (tp % 4 + dy) % 4
+        wide = tbuf[shard * 2 + s].astype(jnp.float32)
+        x = (wide * factors[s, :, :1] * gain[shard]).astype(jnp.bfloat16)
+        depth = x.shape[1]
+        weights = wbuf[pl.ds(2 * shard, 2)].reshape(depth, width)
+        acc[s] += jnp.dot(x, weights, preferred_element_type=jnp.float32)
+
+    def run(js):
+        first, count = js
+
+        def body(i, _):
+            multiply(first + i // 2, i % 2)
+            return 0
+
+        lax.fori_loop(0, 2 * count, body, 0)
+
+    run((0, 5))
+    t["sides"](1)
+    run((5, 1))
+    run((7, 1))
+    t["last"](0)
+    t["last"](1)
+    run((6, 1))
+    for s in range(2):
+        c, d = cosine[s], sine[s]
+        for h in range(width // HEAD_DIM):
+            x = acc[s, :, h * HEAD_DIM:(h + 1) * HEAD_DIM]
+            if h < width // HEAD_DIM - 1:
+                x = x * c + pltpu.roll(x, HEAD_DIM // 2, 1) * d
+            x = x.astype(jnp.bfloat16)
+            if h < qw // HEAD_DIM:
+                q_out[s, h] = x
+            else:
+                kv_out[h - qw // HEAD_DIM, s] = x
+    links.finish()
+
+
+def project(tokens, gain, cosine, sine, wq, wk, wv):
+    n_ctx, n_tp = 16, 8
+    seqs, rows, depth = tokens.shape
+    width = wq.shape[1] + wk.shape[1] + wv.shape[1]
+    bf16, f32 = jnp.bfloat16, jnp.float32
+    heads = wq.shape[1] // HEAD_DIM
+    anyspace = pl.BlockSpec(memory_space=pl.ANY)
+    vmem = pl.BlockSpec(memory_space=pltpu.VMEM)
+    return pl.pallas_call(
+        project_kernel,
+        out_shape=(
+            jax.ShapeDtypeStruct((seqs, heads, rows, HEAD_DIM), bf16),
+            jax.ShapeDtypeStruct((2, seqs, rows, HEAD_DIM), bf16),
+        ),
+        in_specs=[anyspace] * 4 + [vmem] * 3,
+        out_specs=(vmem, vmem),
+        scratch_shapes=[
+            pltpu.VMEM((n_tp * seqs, rows, depth), bf16),
+            pltpu.VMEM((n_ctx, wq.shape[0], width), bf16),
+            pltpu.VMEM((seqs, rows, width), f32),
+            pltpu.VMEM((n_tp, seqs, 8, rows), f32),
+            pltpu.VMEM((seqs, rows, 128), f32),
+            pltpu.SemaphoreType.DMA((44,)),
+            pltpu.SemaphoreType.DMA((44,)),
+            pltpu.SemaphoreType.DMA((4,)),
+        ],
+        compiler_params=pltpu.CompilerParams(
+            collective_id=0, has_side_effects=True, vmem_limit_bytes=48 * 2**20
+        ),
+    )(tokens, wq, wk, wv, gain, cosine, sine)
 
 
 def per_device(tokens, norm_gain, span_order, w_query, w_key, value_weight, w_out):
@@ -59,8 +392,6 @@
     total_rows = sequence_batch * rows_dev
     factor = 1.0 / math.sqrt(head_size)
     rank = lax.axis_index("ctx")
-    whole = lax.all_gather(tokens, "tp", axis=2, tiled=True)
-    normed = normalize(whole.reshape(total_rows, whole.shape[2]), norm_gain)
     query_pos = positions_of(span_order, rank * rows_dev, rows_dev, block_rows)
     latest = jnp.max(query_pos, axis=1)
     stat_shape = (sequence_batch, key_heads, group_width, rows_dev)
@@ -69,22 +400,10 @@
         jnp.zeros(stat_shape, jnp.float32),
         jnp.zeros(stat_shape + (head_size,), jnp.float32),
     )
-    pieces = in_one_piece((w_query, w_key, value_weight), "ctx", 0, 1)
-    query_flat, flattened_key, flattened_value = tuple(
-        (jnp.dot(normed, piece, preferred_element_type=jnp.float32) for piece in pieces)
-    )
-    turned = apply_rotation(
-        query_flat.reshape(sequence_batch, rows_dev, query_heads, head_size), query_pos, head_size
-    ).astype(jnp.bfloat16)
-    query = turned.reshape(sequence_batch, rows_dev, key_heads, group_width, head_size).transpose(
-        0, 2, 3, 1, 4
-    )
-    turned = apply_rotation(
-        flattened_key.reshape(sequence_batch, rows_dev, key_heads, head_size), query_pos, head_size
-    ).astype(jnp.bfloat16)
-    own_values = flattened_value.reshape(sequence_batch, rows_dev, key_heads, head_size).astype(
-        jnp.bfloat16
-    )
+    cosine, sine = angles(query_pos)
+    query, kv = project(tokens, norm_gain.reshape(-1, 1, tokens.shape[2]), cosine, sine, w_query, w_key, value_weight)
+    query = query.reshape(sequence_batch, key_heads, group_width, rows_dev, head_size)
+    turned, own_values = kv[0][:, :, None], kv[1][:, :, None]
     key_piece, value_piece = in_one_piece((turned, own_values), "ctx", 1, 0)
     count = key_piece.shape[1]
     step_rows = 512

time: 455 us -> 326 us (0.72)
  waiting for transfers between devices: 316 us -> 150 us
  Pallas kernels: 0 us -> 82.7 us
  matrix products: 69.2 us -> 38 us
  local copies, waits for them, and re-layouts: 22.2 us -> 11.6 us
    all_gather x1 -> x0, waiting for transfers between devices: 107 us -> none  [per_device(): whole = lax.all_gather(tokens, 'tp', axis=2, tiled=True)]
    pallas_call x0 -> x1, Pallas kernels: none -> 82.7 us  [project(): pl.pallas_call(project_kernel, out_shape=(jax.ShapeDtypeStruct((seqs, hea...]
    all_gather x2 -> x1, waiting for transfers between devices: 93.1 us -> 35.2 us  [in_one_piece(): lax.all_gather(both, axis, axis=dim, tiled=True)]
    dot_general x3 -> x0, matrix products: 23.8 us -> none  [per_device(): jnp.dot(normed, piece, preferred_element_type=jnp.float32)]
    split x2 -> x1, local copies, waits for them, and re-layouts: 11.6 us -> 3.82 us  [in_one_piece(): jnp.split(lax.all_gather(both, axis, axis=dim, tiled=True), ends, axis=al...]
    dot_general x8, matrix products: 14.2 us -> 6.53 us  [update(): jnp.einsum('shgqd,skhd->shgqk', query, key_block, preferred_element_type=...]
    while x11 -> x8, local copies, waits for them, and re-layouts: 6.79 us -> 0.02 us  [the longest x3 6.76 us: per_device(): lax.fori_loop(0, count // step_rows, one_block, initial)]
    reduce_sum x1 -> x0, other arithmetic: 5.1 us -> none  [normalize(): factor = lax.rsqrt(jnp.mean(wide * wide, axis=-1, keepdims=True) + norm_eps)]
  transfers between devices with their start and end apart: 5 -> 3, of which waited for: 4 -> 2; matrix products, arithmetic and copies ran while one was open for 20% -> 16% of each run, Pallas kernels for 0% -> 0%
where the time goes in v1:
time: 326 us; the launch traced here: 325 us
  waiting for transfers between devices  150 us (46%)
  Pallas kernels  82.7 us (25%)
  matrix products  38 us (12%)
  other arithmetic  22.4 us (7%)
  between operations  13.2 us (4%)
  local copies, waits for them, and re-layouts  11.6 us (4%)
  loops' own time  6.49 us (2%)
    reduce_scatter x1, waiting for transfers between devices, per_device(): lax.psum_scatter(terms.astype(jnp.bfloat16), 'tp', scatter_dimension=1, t...  114 us
    pallas_call x1, Pallas kernels, project(): pl.pallas_call(project_kernel, out_shape=(jax.ShapeDtypeStruct((seqs, hea...  82.7 us
    all_gather x1, waiting for transfers between devices, in_one_piece(): lax.all_gather(both, axis, axis=dim, tiled=True)  35.2 us
    dot_general x8, matrix products, update(): jnp.einsum('shgqk,skhd->shgqd', weights.astype(jnp.bfloat16), value_block...  21.4 us
    dot_general x1, matrix products, per_device(): jnp.dot(attended, lax.all_gather(w_out, 'ctx', axis=1, tiled=True), prefe...  10.1 us
    reduce_sum x8, other arithmetic, update(): total = total * shrink + jnp.sum(weights, axis=-1)  8.42 us
    dot_general x8, matrix products, update(): jnp.einsum('shgqd,skhd->shgqk', query, key_block, preferred_element_type=...  6.53 us
  transfers between devices with their start and end apart: 3, of which 2 were waited for; matrix products, arithmetic and copies ran while one was open for 16% of the time, Pallas kernels for 0%

profile of v1, /device:TPU:0, one launch (start us, length us, event | category | flops | bytes accessed | tf_op | source)
XLA Modules:
  0.0 324.9 jit_solution(7795695018402979178)
XLA Ops:
  6.6 0.8 select_reduce_fusion.1
  7.4 1.0 fusion.30
  8.7 1.2 copy-done
  9.9 1.0 copy-done.1
  10.9 0.9 copy-done.2
  11.8 0.9 copy-done.3
  12.7 0.8 copy-done.4
  13.5 82.7 %shard_map.73 = (bf16[2,4,256,128]{3,2,1,0:T(8,128)(2,1)S(1)}, bf16[2,2,256,128]{3,2,1,0:T(8,128)(2,1)S(1)}) custom-call(bf16[2,256,1024]{2,1,0:T(8,128)(2,1)S(1)} %copy-done, bf16[512,512]{1,0:T(8,128)(2,1)S(1)} %copy-done.1, bf16[512,128]{1,0:T(8,128)(2,1)S(1)} %copy-done.2, bf16[512,128]{1,0:T(8,128)(2,1)S(1)} %copy-done.3, f32[8,1,1024]{2,1,0:T(1,128)S(1)} %bitcast.63, ...), custom_call_target="tpu_custom_call" | custom-call | tf_op jit(solution)/shard_map/pallas_call | solution.py:361
  96.2 0.7 pad_maximum_fusion.2
  97.0 0.7 all-gather.5.cloned.1.call-update
  97.7 0.2 reduce-scatter.2.cloned.1.call-start
  98.1 35.2 %all-gather.3.cloned.1.call-done = bf16[4,4096,1,128]{3,1,0,2:T(8,128)(2,1)} async-done(((bf16[4,256,1,128]{3,1,0,2:T(8,128)(2,1)}), bf16[4,4096,1,128]{3,1,0,2:T(8,128)(2,1)}) %all-gather.3.cloned.1.call-update) | async-done | bytes 4194320 | tf_op jit(solution)/shard_map/all_gather | solution.py:24
  133.3 3.8 %fusion.34 = (bf16[2,4096,1,128]{3,1,0,2:T(8,128)(2,1)}, bf16[2,4096,1,128]{3,1,0,2:T(8,128)(2,1)S(1)}) fusion(bf16[4,4096,1,128]{3,1,0,2:T(8,128)(2,1)} %all-gather.3.cloned.1.call-done), kind=kLoop, calls=%fused_computation.66 | loop fusion | bytes 8388608 | tf_op jit(solution)/shard_map/split | solution.py:24
  137.1 1.1 broadcast_in_dim.124
  138.1 53.8 %while.19 = (s32[]{:T(128)}, f32[2,1,4,256]{3,2,0,1:T(4,128)S(1)}, f32[2,1,4,256]{3,2,0,1:T(4,128)S(1)}, f32[2,1,4,256,128]{4,3,2,0,1:T(8,128)}, s32[2,32]{1,0:T...) while((s32[]{:T(128)}, f32[2,1,4,256]{3,2,0,1:T(4,128)S(1)}, ...), condition=%wide.region_10.11_spmd, body=%wide.region_2.10_spmd.sunk | while | flops 551389184 | bytes 25356924 | solution.py:443
  138.4 0.7 compare_reduce_fusion.2
  139.8 5.0 %conditional.2 = (f32[2,1,4,256]{3,2,0,1:T(4,128)S(1)}, f32[2,1,4,256]{3,2,0,1:T(4,128)S(1)}, f32[2,1,4,256,128]{4,3,2,0,1:T(8,128)}) conditional(s32[]{:T(128)} %convert_element_type.45, (s32[2,512]{1,0:T(2,128)S(1)}, s32[2,256]{1,0:T(2,128)S(1)}, s32[]{:T(128)}, bf16[2,4096,1,128]{3,1,0,2:T(8,128)(2,1)S(1)}, ...), branch_computations={%region_6.8_spmd, %region_9.9_spmd} | conditional | flops 551294976 | bytes 25286778 | solution.py:439
  139.8 0.2 broadcast_compare_fusion
  140.0 0.8 fusion
  141.0 2.7 fusion.9
  143.7 1.1 fusion.2
  145.1 0.7 compare_reduce_fusion.2
  146.5 5.0 %conditional.2 = (f32[2,1,4,256]{3,2,0,1:T(4,128)S(1)}, f32[2,1,4,256]{3,2,0,1:T(4,128)S(1)}, f32[2,1,4,256,128]{4,3,2,0,1:T(8,128)}) conditional(s32[]{:T(128)} %convert_element_type.45, (s32[2,512]{1,0:T(2,128)S(1)}, s32[2,256]{1,0:T(2,128)S(1)}, s32[]{:T(128)}, bf16[2,4096,1,128]{3,1,0,2:T(8,128)(2,1)S(1)}, ...), branch_computations={%region_6.8_spmd, %region_9.9_spmd} | conditional | flops 551294976 | bytes 25286778 | solution.py:439
  146.5 0.2 broadcast_compare_fusion
  146.8 0.8 fusion
  147.8 2.7 fusion.9
  150.4 1.1 fusion.2
  151.8 0.7 compare_reduce_fusion.2
  153.2 5.0 %conditional.2 = (f32[2,1,4,256]{3,2,0,1:T(4,128)S(1)}, f32[2,1,4,256]{3,2,0,1:T(4,128)S(1)}, f32[2,1,4,256,128]{4,3,2,0,1:T(8,128)}) conditional(s32[]{:T(128)} %convert_element_type.45, (s32[2,512]{1,0:T(2,128)S(1)}, s32[2,256]{1,0:T(2,128)S(1)}, s32[]{:T(128)}, bf16[2,4096,1,128]{3,1,0,2:T(8,128)(2,1)S(1)}, ...), branch_computations={%region_6.8_spmd, %region_9.9_spmd} | conditional | flops 551294976 | bytes 25286778 | solution.py:439
  153.3 0.2 broadcast_compare_fusion
  153.5 0.8 fusion
  154.5 2.7 fusion.9
  157.2 1.1 fusion.2
  158.5 0.7 compare_reduce_fusion.2
  159.9 5.0 %conditional.2 = (f32[2,1,4,256]{3,2,0,1:T(4,128)S(1)}, f32[2,1,4,256]{3,2,0,1:T(4,128)S(1)}, f32[2,1,4,256,128]{4,3,2,0,1:T(8,128)}) conditional(s32[]{:T(128)} %convert_element_type.45, (s32[2,512]{1,0:T(2,128)S(1)}, s32[2,256]{1,0:T(2,128)S(1)}, s32[]{:T(128)}, bf16[2,4096,1,128]{3,1,0,2:T(8,128)(2,1)S(1)}, ...), branch_computations={%region_6.8_spmd, %region_9.9_spmd} | conditional | flops 551294976 | bytes 25286778 | solution.py:439
  160.0 0.2 broadcast_compare_fusion
  160.2 0.8 fusion
  161.2 2.7 fusion.9
  163.9 1.1 fusion.2
  165.3 0.7 compare_reduce_fusion.2
  166.7 5.0 %conditional.2 = (f32[2,1,4,256]{3,2,0,1:T(4,128)S(1)}, f32[2,1,4,256]{3,2,0,1:T(4,128)S(1)}, f32[2,1,4,256,128]{4,3,2,0,1:T(8,128)}) conditional(s32[]{:T(128)} %convert_element_type.45, (s32[2,512]{1,0:T(2,128)S(1)}, s32[2,256]{1,0:T(2,128)S(1)}, s32[]{:T(128)}, bf16[2,4096,1,128]{3,1,0,2:T(8,128)(2,1)S(1)}, ...), branch_computations={%region_6.8_spmd, %region_9.9_spmd} | conditional | flops 551294976 | bytes 25286778 | solution.py:439
  166.9 0.8 fusion
  167.9 2.7 fusion.9
  170.6 1.1 fusion.2
  172.0 0.7 compare_reduce_fusion.2
  173.4 5.1 %conditional.2 = (f32[2,1,4,256]{3,2,0,1:T(4,128)S(1)}, f32[2,1,4,256]{3,2,0,1:T(4,128)S(1)}, f32[2,1,4,256,128]{4,3,2,0,1:T(8,128)}) conditional(s32[]{:T(128)} %convert_element_type.45, (s32[2,512]{1,0:T(2,128)S(1)}, s32[2,256]{1,0:T(2,128)S(1)}, s32[]{:T(128)}, bf16[2,4096,1,128]{3,1,0,2:T(8,128)(2,1)S(1)}, ...), branch_computations={%region_6.8_spmd, %region_9.9_spmd} | conditional | flops 551294976 | bytes 25286778 | solution.py:439
  173.6 0.8 fusion
  174.7 2.7 fusion.9
  177.4 1.1 fusion.2
  178.8 0.7 compare_reduce_fusion.2
  180.1 5.1 %conditional.2 = (f32[2,1,4,256]{3,2,0,1:T(4,128)S(1)}, f32[2,1,4,256]{3,2,0,1:T(4,128)S(1)}, f32[2,1,4,256,128]{4,3,2,0,1:T(8,128)}) conditional(s32[]{:T(128)} %convert_element_type.45, (s32[2,512]{1,0:T(2,128)S(1)}, s32[2,256]{1,0:T(2,128)S(1)}, s32[]{:T(128)}, bf16[2,4096,1,128]{3,1,0,2:T(8,128)(2,1)S(1)}, ...), branch_computations={%region_6.8_spmd, %region_9.9_spmd} | conditional | flops 551294976 | bytes 25286778 | solution.py:439
  180.4 0.8 fusion
  181.2 0.2 copy-done.5
  181.5 2.7 fusion.9
  184.1 1.1 fusion.2
  185.5 0.7 compare_reduce_fusion.2
  186.9 5.0 %conditional.2 = (f32[2,1,4,256]{3,2,0,1:T(4,128)S(1)}, f32[2,1,4,256]{3,2,0,1:T(4,128)S(1)}, f32[2,1,4,256,128]{4,3,2,0,1:T(8,128)}) conditional(s32[]{:T(128)} %convert_element_type.45, (s32[2,512]{1,0:T(2,128)S(1)}, s32[2,256]{1,0:T(2,128)S(1)}, s32[]{:T(128)}, bf16[2,4096,1,128]{3,1,0,2:T(8,128)(2,1)S(1)}, ...), branch_computations={%region_6.8_spmd, %region_9.9_spmd} | conditional | flops 551294976 | bytes 25286778 | solution.py:439
  187.2 0.8 fusion
  188.2 2.7 fusion.9
  190.9 1.1 fusion.2
  192.0 1.6 fusion.29
  193.5 0.4 copy.12
  194.0 10.1 %convolution_convert_fusion = bf16[512,8192]{1,0:T(8,128)(2,1)} fusion(bf16[512,8192]{1,0:T(8,128)(2,1)} %all-gather.5.cloned.1.call-done, bf16[64,8,4,128]{3,2,1,0:T(4,128)(2,1)S(1)} %bitcast.67), kind=kOutput, calls=%fused_computation.39 | convolution fusion | flops 4299161600 | bytes 17301504 | tf_op jit(solution)/shard_map/dot_general | solution.py:446
  204.1 114.2 %reduce-scatter.2.cloned.1.call-done = bf16[512,1024]{1,0:T(8,128)(2,1)} async-done(((bf16[512,8192]{1,0:T(8,128)(2,1)}), bf16[512,1024]{1,0:T(8,128)(2,1)}) %reduce-scatter.2.cloned.1.call-update) | async-done | bytes 1048592 | tf_op jit(solution)/shard_map/reduce_scatter | solution.py:451
  (113 shorter events, 4.9 us)
Async XLA Ops:
  6.5 126.7 %all-gather.3.cloned.1.call-start = ((), (), s32[]{:S(2)}) async-start(), calls=%async_computation.1 | async-start | bytes 4456448 | tf_op jit(solution)/shard_map/all_gather | solution.py:24
  8.6 1.2 copy-start
  9.9 1.0 copy-start.1
  10.9 0.9 copy-start.2
  11.8 0.9 copy-start.3
  12.7 0.8 copy-start.4
  97.0 97.0 %all-gather.5.cloned.1.call-start = ((), (), s32[]{:S(2)}) async-start(), calls=%async_computation.2 | async-start | bytes 8912896 | tf_op jit(solution)/shard_map/all_gather | solution.py:448
  97.7 220.6 %reduce-scatter.2.cloned.1.call-start = ((), (), s32[]{:S(2)}) async-start(), calls=%async_computation.3 | async-start | bytes 9437184 | tf_op jit(solution)/shard_map/reduce_scatter | solution.py:451
  98.1 40.1 %copy-start.7 = (s32[2,32]{1,0:T(2,128)S(1)}, s32[2,32]{1,0:T(2,128)}, u32[]{:S(2)}) copy-start(s32[2,32]{1,0:T(2,128)} %param.13) | copy-start | bytes 772
  139.8 1.2 copy-start.5
  143.7 1.1 copy-start.6
  146.5 1.2 copy-start.5
  150.4 1.1 copy-start.6
  153.2 1.2 copy-start.5
  157.1 1.1 copy-start.6
  160.0 1.2 copy-start.5
  163.9 1.1 copy-start.6
  166.7 1.2 copy-start.5
  170.6 1.1 copy-start.6
  173.4 1.3 copy-start.5
  177.4 1.1 copy-start.6
  180.2 1.3 copy-start.5
  184.1 1.1 copy-start.6
  186.9 1.2 copy-start.5
  190.8 1.1 copy-start.6
Sparse Core Ops, SparseCore 0:
  97.1 36.1 all-gather.2
  134.9 51.9 all-gather.4
  204.2 114.0 reduce-scatter.1

commit v2 on v1

v2 whole, which is shorter than its diff:
```python
import math

import jax
import jax.numpy as jnp
from jax import lax
from jax.experimental import pallas as pl
from jax.experimental.pallas import tpu as pltpu
from jax.sharding import PartitionSpec as P

HEAD_DIM = 128


theta_base = 500000.0
norm_eps = 1e-05
masked_score = -1e30


def in_one_piece(arrays, axis, dim, along):
    ends, at = ([], 0)
    for a in arrays[:-1]:
        at += a.shape[along]
        ends.append(at)
    both = jnp.concatenate(arrays, axis=along)
    return tuple(jnp.split(lax.all_gather(both, axis, axis=dim, tiled=True), ends, axis=along))


def angles(token_position):
    half = HEAD_DIM // 2
    freqs = jnp.exp(-(2.0 * jnp.arange(half, dtype=jnp.float32) / HEAD_DIM) * math.log(theta_base))
    angle = token_position.astype(jnp.float32)[..., None] * freqs
    cosine, sine = jnp.cos(angle), jnp.sin(angle)
    return jnp.concatenate([cosine, cosine], axis=-1), jnp.concatenate([-sine, sine], axis=-1)


MESH = pl.DeviceIdType.MESH


def neighbours():
    ctx, tp = lax.axis_index("ctx"), lax.axis_index("tp")
    z, xl, core = ctx // 4, (ctx // 2) % 2, ctx % 2
    xh, y = tp // 4, tp % 4

    def at(z_, xl_, core_, xh_, y_):
        return {"ctx": z_ * 4 + xl_ * 2 + core_, "tp": xh_ * 4 + y_}

    return {
        "yp": at(z, xl, core, xh, (y + 1) % 4),
        "ym": at(z, xl, core, xh, (y + 3) % 4),
        "y2": at(z, xl, core, xh, (y + 2) % 4),
        "xh": at(z, xl, core, 1 - xh, y),
        "xhyp": at(z, xl, core, 1 - xh, (y + 1) % 4),
        "xhym": at(z, xl, core, 1 - xh, (y + 3) % 4),
        "xhy2": at(z, xl, core, 1 - xh, (y + 2) % 4),
        "zp": at((z + 1) % 4, xl, core, xh, y),
        "zm": at((z + 3) % 4, xl, core, xh, y),
        "xl": at(z, 1 - xl, core, xh, y),
        "co": at(z, xl, 1 - core, xh, y),
    }


class Links:
    def __init__(self, send, recv):
        self.send, self.recv, self.count = send, recv, 0
        self.where = neighbours()
        self.sent = []

    def greet(self, names):
        barrier = pltpu.get_barrier_semaphore()
        for name in names:
            pl.semaphore_signal(barrier, 1, device_id=self.where[name], device_id_type=MESH)
        pl.semaphore_wait(barrier, len(names))

    def ticket(self):
        self.count += 1
        return self.count - 1

    def copy(self, ticket, src, dst, name):
        return pltpu.make_async_remote_copy(
            src, dst, self.send.at[ticket], self.recv.at[ticket],
            device_id=self.where[name], device_id_type=MESH,
        )

    def start(self, ticket, src, dst, name):
        c = self.copy(ticket, src, dst, name)
        c.start()
        self.sent.append(c)

    def arrive(self, ticket, here, name="co"):
        self.copy(ticket, here, here, name).wait_recv()

    def finish(self):
        for c in self.sent:
            c.wait_send()
        self.sent = []


def token_flow(links, tokens_buf, source):
    tp = lax.axis_index("tp")
    xh, y = tp // 4, tp % 4

    def shard(dx, dy):
        return (xh if dx == 0 else 1 - xh) * 4 + (y + dy) % 4

    def slot(dx, dy, s, rows=None):
        ref = tokens_buf.at[shard(dx, dy) * 2 + s]
        return ref if rows is None else ref.at[pl.ds(rows[0], rows[1])]

    rows = tokens_buf.shape[1]
    low, high = (0, rows // 2), (rows // 2, rows // 2)
    T = {}
    for s in range(2):
        for k in ("yp", "ym", "xh", "fa", "fb", "pyp", "pym", "x2"):
            T[k, s] = links.ticket()

    def own(s):
        links.start(T["xh", s], source.at[s], slot(0, 0, s), "xh")
        links.start(T["yp", s], source.at[s], slot(0, 0, s), "yp")
        links.start(T["ym", s], source.at[s], slot(0, 0, s), "ym")

    def forward(s):
        links.arrive(T["yp", s], slot(0, 3, s), "ym")
        links.start(T["fa", s], slot(0, 3, s, low), slot(0, 3, s, low), "yp")
        links.arrive(T["ym", s], slot(0, 1, s), "yp")
        links.start(T["fb", s], slot(0, 1, s, high), slot(0, 1, s, high), "ym")

    def partner(s):
        links.arrive(T["xh", s], slot(1, 0, s), "xh")
        links.start(T["pyp", s], slot(1, 0, s), slot(1, 0, s), "yp")
        links.start(T["pym", s], slot(1, 0, s), slot(1, 0, s), "ym")

    def across(s):
        links.arrive(T["fa", s], slot(0, 2, s, low), "ym")
        links.arrive(T["fb", s], slot(0, 2, s, high), "yp")
        links.start(T["x2", s], slot(0, 2, s), slot(0, 2, s), "xh")

    def sides(s):
        links.arrive(T["pyp", s], slot(1, 3, s), "ym")
        links.arrive(T["pym", s], slot(1, 1, s), "yp")

    def last(s):
        links.arrive(T["x2", s], slot(1, 2, s), "xh")

    return dict(own=own, forward=forward, partner=partner, across=across, sides=sides, last=last, shard=shard)


def squares_flow(links, buf):
    tp = lax.axis_index("tp")
    xh, y = tp // 4, tp % 4

    def slot(dx, dy):
        return buf.at[(xh if dx == 0 else 1 - xh) * 4 + (y + dy) % 4]

    routes = {"yp": (0, 3), "ym": (0, 1), "y2": (0, 2), "xh": (1, 0), "xhyp": (1, 3), "xhym": (1, 1), "xhy2": (1, 2)}
    T = {k: links.ticket() for k in routes}

    def own():
        for k in routes:
            links.start(T[k], slot(0, 0), slot(0, 0), k)

    def arrived():
        for k, where in routes.items():
            links.arrive(T[k], slot(*where))

    return {"own": own, "all": arrived}


def by_rank(z, xl, core):
    return z * 4 + xl * 2 + core


def by_pair(z, xl, core):
    return xl * 8 + z * 2 + core


def column_flow(links, buf, place=by_rank):
    ctx = lax.axis_index("ctx")
    z, xl, core = ctx // 4, (ctx // 2) % 2, ctx % 2
    rows = buf.shape[1]
    half = rows // 2

    def slot(dx, dz, dc=0, part=None):
        i = place((z + dz) % 4, xl if dx == 0 else 1 - xl, core if dc == 0 else 1 - core)
        ref = buf.at[i]
        return ref if part is None else ref.at[pl.ds(part * half, half)]

    T = {}
    for k in ("zp", "zm", "xl0", "xl1", "fa", "fb", "pzp0", "pzp1", "pzm0", "pzm1", "pfa", "pfb"):
        T[k] = links.ticket()
    for dx in range(2):
        for dz in range(4):
            T["co", dx, dz] = links.ticket()

    def share(dx, dz):
        links.start(T["co", dx, dz], slot(dx, dz), slot(dx, dz), "co")

    def own_x(part):
        links.start(T[f"xl{part}"], slot(0, 0, 0, part), slot(0, 0, 0, part), "xl")

    def own_z():
        links.start(T["zp"], slot(0, 0), slot(0, 0), "zp")
        links.start(T["zm"], slot(0, 0), slot(0, 0), "zm")
        share(0, 0)

    def forward():
        links.arrive(T["zp"], slot(0, 3), "zm")
        links.start(T["fa"], slot(0, 3, 0, 0), slot(0, 3, 0, 0), "zp")
        links.arrive(T["zm"], slot(0, 1), "zp")
        links.start(T["fb"], slot(0, 1, 0, 1), slot(0, 1, 0, 1), "zm")
        share(0, 3)
        share(0, 1)

    def partner(part):
        links.arrive(T[f"xl{part}"], slot(1, 0, 0, part), "xl")
        links.start(T[f"pzp{part}"], slot(1, 0, 0, part), slot(1, 0, 0, part), "zp")
        links.start(T[f"pzm{part}"], slot(1, 0, 0, part), slot(1, 0, 0, part), "zm")
        if part == 1:
            share(1, 0)

    def across():
        links.arrive(T["fa"], slot(0, 2, 0, 0), "zm")
        links.arrive(T["fb"], slot(0, 2, 0, 1), "zp")
        share(0, 2)

    def sides():
        links.arrive(T["pzp0"], slot(1, 3, 0, 0), "zm")
        links.start(T["pfa"], slot(1, 3, 0, 0), slot(1, 3, 0, 0), "zp")
        links.arrive(T["pzm0"], slot(1, 1, 0, 0), "zp")
        links.arrive(T["pzm1"], slot(1, 1, 0, 1), "zp")
        links.start(T["pfb"], slot(1, 1, 0, 1), slot(1, 1, 0, 1), "zm")
        links.arrive(T["pzp1"], slot(1, 3, 0, 1), "zm")
        share(1, 3)
        share(1, 1)

    def last():
        links.arrive(T["pfa"], slot(1, 2, 0, 0), "zm")
        links.arrive(T["pfb"], slot(1, 2, 0, 1), "zp")
        share(1, 2)

    def shared(pairs):
        for dx, dz in pairs:
            links.arrive(T["co", dx, dz], slot(dx, dz, 1), "co")

    everything = [(dx, dz) for dx in range(2) for dz in range(4)]
    return dict(own_x=own_x, own_z=own_z, forward=forward, partner=partner, across=across, sides=sides,
                last=last, shared=shared, everything=everything)


def attend(first_pair, pair, q_buf, kv_buf, query_pos, key_pos, peaks, sums, out):
    rows = q_buf.shape[1]
    heads = out.shape[2] // HEAD_DIM
    scale = math.log2(math.e) / math.sqrt(HEAD_DIM)

    def body(i, _):
        s, h = i // heads, i % heads
        at = pl.multiple_of(s * rows, rows)
        keys = kv_buf[pl.ds(pair * 8, 8), pl.ds(at, rows), :].reshape(8 * rows, HEAD_DIM)
        values = kv_buf[pl.ds(pair * 8, 8), pl.ds(2 * rows + at, rows), :].reshape(8 * rows, HEAD_DIM)
        scores = lax.dot_general(
            q_buf[i], keys, (((1,), (1,)), ((), ())), preferred_element_type=jnp.float32
        )
        allowed = key_pos[s * 2 + pair] <= query_pos[s, :, :1]
        scores = jnp.where(allowed, scores, masked_score)
        peak = jnp.maximum(jnp.max(scores, axis=1, keepdims=True), 1e-10 * masked_score)
        if not first_pair:
            before = peaks[i, :, :1]
            peak = jnp.maximum(peak, before)
        weights = jnp.exp2((scores - peak) * scale).astype(jnp.bfloat16)
        both = jnp.concatenate([values, jnp.ones_like(values)], axis=1)
        summed = jnp.dot(weights, both, preferred_element_type=jnp.float32)
        if first_pair:
            peaks[i] = jnp.broadcast_to(peak, peaks.shape[1:])
            sums[i] = summed
        else:
            summed = summed + sums[i] * jnp.exp2((before - peak) * scale)
            mean = summed[:, :HEAD_DIM] / summed[:, HEAD_DIM:]
            out[s, :, pl.ds(pl.multiple_of(h * HEAD_DIM, HEAD_DIM), HEAD_DIM)] = mean.astype(jnp.bfloat16)
        return 0

    lax.fori_loop(0, 2 * heads, body, 0)


def mix_kernel(tokens, wq, wk, wv, wo, gain, cosine, sine, query_pos, key_pos, mixed,
               tbuf, wbuf, acc, squares, factors, wobuf, kvbuf, qbuf, peaks, sums, attended,
               terms, from_x, from_y, halves, last_y, last_x, send, recv, local):
    links = Links(send, recv)
    ctx, tp = lax.axis_index("ctx"), lax.axis_index("tp")
    z, xl, core = ctx // 4, (ctx // 2) % 2, ctx % 2
    rows = tokens.shape[1]
    qw, kw = wq.shape[1], wk.shape[1]
    width = qw + 2 * kw
    heads = qw // HEAD_DIM
    mine = [
        pltpu.make_async_copy(wq, wbuf.at[ctx, :, pl.ds(0, qw)], local.at[0]),
        pltpu.make_async_copy(wk, wbuf.at[ctx, :, pl.ds(qw, kw)], local.at[1]),
        pltpu.make_async_copy(wv, wbuf.at[ctx, :, pl.ds(qw + kw, kw)], local.at[2]),
        pltpu.make_async_copy(tokens, tbuf.at[pl.ds(tp * 2, 2)], local.at[3]),
        pltpu.make_async_copy(wo, wobuf.at[ctx], local.at[4]),
    ]
    for c in (mine[3], *mine[:3], mine[4]):
        c.start()
    t = token_flow(links, tbuf, tokens)
    w = column_flow(links, wbuf)
    statistics = squares_flow(links, squares)
    o = column_flow(links, wobuf)
    kv = column_flow(links, kvbuf, by_pair)
    mine[3].wait()
    for s in range(2):
        wide = tbuf[tp * 2 + s].astype(jnp.float32)
        squares[tp, s] = lax.dot_general(
            jnp.ones((8, wide.shape[1]), jnp.float32), wide * wide, (((1,), (1,)), ((), ())),
            precision=lax.Precision.HIGHEST, preferred_element_type=jnp.float32,
        )
    for c in mine[:3]:
        c.wait()
    links.greet(("yp", "ym", "y2", "xh", "xhyp", "xhym", "xhy2", "zp", "zm", "xl", "co"))
    statistics["own"]()
    w["own_x"](0)
    t["own"](0)
    w["own_z"]()
    w["own_x"](1)
    t["own"](1)
    acc[...] = jnp.zeros_like(acc)
    mine[4].wait()

    t["forward"](0)
    w["forward"]()
    w["partner"](0)
    t["partner"](0)
    t["forward"](1)
    w["partner"](1)
    w["across"]()
    t["across"](0)
    t["partner"](1)
    t["across"](1)
    o["own_x"](0)
    o["own_x"](1)
    statistics["all"]()
    features = 8 * tokens.shape[2]
    for s in range(2):
        total = squares[0, s]
        for i in range(1, 8):
            total = total + squares[i, s]
        factor = lax.rsqrt(total[:1] * (1.0 / features) + norm_eps)
        factors[s] = jnp.transpose(jnp.broadcast_to(factor, (128, rows)))
    w["sides"]()
    o["own_z"]()
    t["sides"](0)
    w["last"]()
    w["shared"](w["everything"])

    def multiply(j, s):
        dx, dy = j // 4, j % 4
        shard = (tp // 4 + dx) % 2 * 4 + (tp % 4 + dy) % 4
        wide = tbuf[shard * 2 + s].astype(jnp.float32)
        x = (wide * factors[s, :, :1] * gain[shard]).astype(jnp.bfloat16)
        weights = wbuf[pl.ds(2 * shard, 2)].reshape(x.shape[1], width)
        acc[s] += jnp.dot(x, weights, preferred_element_type=jnp.float32)

    def run(first, count):
        def body(i, _):
            multiply(first + i // 2, i % 2)
            return 0

        lax.fori_loop(0, 2 * count, body, 0)

    run(0, 5)
    o["forward"]()
    t["sides"](1)
    run(5, 1)
    run(7, 1)
    o["across"]()
    t["last"](0)
    t["last"](1)
    run(6, 1)

    own = by_pair(z, xl, core)

    def turn(x, s):
        return x * cosine[s] + pltpu.roll(x, HEAD_DIM // 2, 1) * sine[s]

    for s in range(2):
        kvbuf[own, s * rows:(s + 1) * rows] = turn(acc[s, :, qw:qw + kw], s).astype(jnp.bfloat16)
        kvbuf[own, (2 + s) * rows:(3 + s) * rows] = acc[s, :, qw + kw:].astype(jnp.bfloat16)
    kv["own_x"](0)
    kv["own_z"]()
    kv["own_x"](1)
    for s in range(2):
        for h in range(heads):
            qbuf[s * heads + h] = turn(acc[s, :, h * HEAD_DIM:(h + 1) * HEAD_DIM], s).astype(jnp.bfloat16)
    kv["partner"](0)
    kv["forward"]()
    kv["partner"](1)
    kv["across"]()
    kv["shared"]([(0, dz) for dz in range(4)])
    kv["sides"]()
    o["partner"](0)
    o["partner"](1)
    attend(True, xl, qbuf, kvbuf, query_pos, key_pos, peaks, sums, attended)
    kv["last"]()
    kv["shared"]([(1, dz) for dz in range(4)])
    o["sides"]()
    attend(False, 1 - xl, qbuf, kvbuf, query_pos, key_pos, peaks, sums, attended)
    o["last"]()
    o["shared"](o["everything"])

    half = terms.shape[2]

    def term(dx, dy, c):
        return (dx * 4 + dy) * 2 + c

    def products(first, count):
        def body(i, _):
            rel, c = first + i // 2, i % 2
            block = (tp // 4 + rel // 4) % 2 * 4 + (tp % 4 + rel % 4) % 4
            terms[2 * first + i] = jnp.dot(
                attended[...].reshape(2 * rows, qw), wobuf[2 * block + c], preferred_element_type=jnp.float32
            ).astype(jnp.bfloat16)
            return 0

        lax.fori_loop(0, 2 * count, body, 0)

    R = {}
    for k in ("x", "yp", "ym", "h", "zyp", "zym", "zx"):
        for c in range(2):
            R[k, c] = links.ticket()

    def add(index, *others):
        total = terms[index].astype(jnp.float32)
        for ref in others:
            total = total + ref[...].astype(jnp.float32)
        return total

    products(6, 1)
    for c in range(2):
        links.start(R["x", c], terms.at[term(1, 2, c)], from_x.at[c], "xh")
    products(5, 1)
    for c in range(2):
        links.start(R["yp", c], terms.at[term(1, 1, c)], from_y.at[c], "yp")
    products(7, 1)
    for c in range(2):
        links.start(R["ym", c], terms.at[term(1, 3, c)], from_y.at[2 + c], "ym")
    products(0, 5)
    for c, to in ((0, "yp"), (1, "ym")):
        links.arrive(R["x", c], from_x.at[c])
        terms[term(0, 2, c)] = add(term(0, 2, c), from_x.at[c]).astype(jnp.bfloat16)
        links.start(R["h", c], terms.at[term(0, 2, c)], halves.at[c], to)
    links.start(R["zyp", 1], terms.at[term(0, 1, 1)], last_y.at[1], "yp")
    links.start(R["zym", 0], terms.at[term(0, 3, 0)], last_y.at[2], "ym")
    for c in range(2):
        links.arrive(R["yp", c], from_y.at[c])
        links.arrive(R["ym", c], from_y.at[2 + c])
        terms[term(1, 0, c)] = add(term(1, 0, c), from_y.at[c], from_y.at[2 + c]).astype(jnp.bfloat16)
        links.start(R["zx", c], terms.at[term(1, 0, c)], last_x.at[c], "xh")
    links.arrive(R["h", 0], halves.at[0])
    terms[term(0, 1, 0)] = add(term(0, 1, 0), halves.at[0]).astype(jnp.bfloat16)
    links.start(R["zyp", 0], terms.at[term(0, 1, 0)], last_y.at[0], "yp")
    links.arrive(R["h", 1], halves.at[1])
    terms[term(0, 3, 1)] = add(term(0, 3, 1), halves.at[1]).astype(jnp.bfloat16)
    links.start(R["zym", 1], terms.at[term(0, 3, 1)], last_y.at[3], "ym")
    for c in range(2):
        links.arrive(R["zx", c], last_x.at[c])
        links.arrive(R["zyp", c], last_y.at[c])
        links.arrive(R["zym", c], last_y.at[2 + c])
        total = add(term(0, 0, c), last_x.at[c], last_y.at[c], last_y.at[2 + c])
        mixed[:, :, c * half:(c + 1) * half] = total.astype(jnp.bfloat16).reshape(2, rows, half)
    links.finish()


def per_device(tokens, norm_gain, span_order, w_query, w_key, value_weight, w_out):
    n_ctx, n_tp = 16, 8
    seqs, rows, depth = tokens.shape
    qw = w_query.shape[1]
    width = qw + w_key.shape[1] + value_weight.shape[1]
    heads = qw // HEAD_DIM
    blocks = span_order.shape[1]
    block_rows = n_ctx * rows // blocks
    bf16, f32 = jnp.bfloat16, jnp.float32
    position = (span_order[:, :, None] * block_rows + jnp.arange(block_rows, dtype=jnp.int32)).reshape(seqs, n_ctx * rows)
    query_pos = lax.dynamic_slice_in_dim(position, lax.axis_index("ctx") * rows, rows, 1)
    cosine, sine = angles(query_pos)
    key_pos = position.reshape(seqs, 4, 2, 2 * rows).transpose(0, 2, 1, 3).reshape(2 * seqs, 1, 8 * rows)
    query_pos = jnp.broadcast_to(query_pos[:, :, None], (seqs, rows, 128))
    anyspace = pl.BlockSpec(memory_space=pl.ANY)
    vmem = pl.BlockSpec(memory_space=pltpu.VMEM)
    half = depth // 2
    return pl.pallas_call(
        mix_kernel,
        out_shape=jax.ShapeDtypeStruct(tokens.shape, bf16),
        in_specs=[anyspace] * 5 + [vmem] * 5,
        out_specs=vmem,
        scratch_shapes=[
            pltpu.VMEM((n_tp * seqs, rows, depth), bf16),
            pltpu.VMEM((n_ctx, w_query.shape[0], width), bf16),
            pltpu.VMEM((seqs, rows, width), f32),
            pltpu.VMEM((n_tp, seqs, 8, rows), f32),
            pltpu.VMEM((seqs, rows, 128), f32),
            pltpu.VMEM((n_ctx, *w_out.shape), bf16),
            pltpu.VMEM((n_ctx, 2 * seqs * rows, HEAD_DIM), bf16),
            pltpu.VMEM((seqs * heads, rows, HEAD_DIM), bf16),
            pltpu.VMEM((seqs * heads, rows, 128), f32),
            pltpu.VMEM((seqs * heads, rows, 2 * HEAD_DIM), f32),
            pltpu.VMEM((seqs, rows, qw), bf16),
            pltpu.VMEM((2 * n_tp, seqs * rows, half), bf16),
            pltpu.VMEM((2, seqs * rows, half), bf16),
            pltpu.VMEM((4, seqs * rows, half), bf16),
            pltpu.VMEM((2, seqs * rows, half), bf16),
            pltpu.VMEM((4, seqs * rows, half), bf16),
            pltpu.VMEM((2, seqs * rows, half), bf16),
            pltpu.SemaphoreType.DMA((104,)),
            pltpu.SemaphoreType.DMA((104,)),
            pltpu.SemaphoreType.DMA((5,)),
        ],
        compiler_params=pltpu.CompilerParams(
            collective_id=0, has_side_effects=True, vmem_limit_bytes=63 * 2**20
        ),
    )(tokens, w_query, w_key, value_weight, w_out, norm_gain.reshape(n_tp, 1, depth), cosine, sine, query_pos, key_pos)


def solution(mesh):
    placed = (
        P(None, "ctx", "tp"),
        P(),
        P(),
        P("ctx", "tp"),
        P("ctx", "tp"),
        P("ctx", "tp"),
        P("tp", "ctx"),
    )
    return jax.shard_map(
        per_device, mesh=mesh, in_specs=placed, out_specs=P(None, "ctx", "tp"), check_vma=False
    )
```

time: 326 us -> 208 us (0.64)
  waiting for transfers between devices: 150 us -> 0 us
  Pallas kernels: 82.7 us -> 200 us
  matrix products: 38 us -> 0 us
  other arithmetic: 22.4 us -> 2.02 us
  between operations: 13.2 us -> 0.06 us
  local copies, waits for them, and re-layouts: 11.6 us -> 4.72 us
  loops' own time: 6.49 us -> 0 us
    pallas_call x1, Pallas kernels: 82.7 us -> 200 us  [per_device(): pl.pallas_call(mix_kernel, out_shape=jax.ShapeDtypeStruct(tokens.shape, b...]
    reduce_scatter x1 -> x0, waiting for transfers between devices: 114 us -> none  [per_device(): lax.psum_scatter(terms.astype(jnp.bfloat16), 'tp', scatter_dimension=1, t...]
    dot_general x17 -> x0, matrix products: 38 us -> none  [the longest x8 21.4 us: update(): jnp.einsum('shgqk,skhd->shgqd', weights.astype(jnp.bfloat16), value_block...]
    all_gather x2 -> x0, waiting for transfers between devices: 35.2 us -> none  [the longest x1 35.2 us: in_one_piece(): lax.all_gather(both, axis, axis=dim, tiled=True)]
    reduce_sum x17 -> x0, other arithmetic: 9.95 us -> none  [the longest x8 8.42 us: update(): total = total * shrink + jnp.sum(weights, axis=-1)]
    another operation x9 -> x0, loops' own time: 6.49 us -> none  [the longest x1 5.87 us: per_device(): lax.fori_loop(0, count // step_rows, one_block, initial)]
    reduce_and x8 -> x0, other arithmetic: 5.66 us -> none  [one_block(): jnp.all(jnp.min(key_pos, axis=1) > latest)]
    split x1 -> x0, local copies, waits for them, and re-layouts: 3.82 us -> none  [in_one_piece(): jnp.split(lax.all_gather(both, axis, axis=dim, tiled=True), ends, axis=al...]
  transfers between devices with their start and end apart: 3 -> 0, of which waited for: 2 -> 0; matrix products, arithmetic and copies ran while one was open for 16% -> 0% of each run, Pallas kernels for 0% -> 0%
where the time goes in v2:
time: 208 us; the launch traced here: 207 us
  Pallas kernels  200 us (96%)
  local copies, waits for them, and re-layouts  4.72 us (2%)
    pallas_call x1, Pallas kernels, per_device(): pl.pallas_call(mix_kernel, out_shape=jax.ShapeDtypeStruct(tokens.shape, b...  200 us

profile of v2, /device:TPU:0, one launch (start us, length us, event | category | flops | bytes accessed | tf_op | source)
XLA Modules:
  0.0 206.7 jit_solution(4806727804922978842)
XLA Ops:
  0.0 0.0 copy-start
  0.0 0.7 copy-done
  0.7 0.1 dynamic-slice
  0.8 0.1 broadcast_bitcast_fusion
  0.9 0.1 add.34
  1.0 0.7 reshape.24.key_pos
  1.7 0.9 broadcast_in_dim.2.query_pos
  2.5 1.0 fusion
  3.5 1.0 pad_maximum_fusion
  4.5 199.9 %shard_map.73 = bf16[2,256,1024]{2,1,0:T(8,128)(2,1)} custom-call(bf16[2,256,1024]{2,1,0:T(8,128)(2,1)} %tokens.1, bf16[512,512]{1,0:T(8,128)(2,1)} %wq.1, bf16[512,128]{1,0:T(8,128)(2,1)} %wk.1, bf16[512,128]{1,0:T(8,128)(2,1)} %wv.1, bf16[512,512]{1,0:T(8,128)(2,1)} %wo.1, f32[8,1,1024]{2,1,0:T(1,128)} %bitcast.13, ...), custom_call_target="tpu_custom_call" | custom-call | tf_op jit(solution)/shard_map/pallas_call | solution.py:486
  204.4 2.3 %copy.13 = bf16[2,256,1024]{2,1,0:T(8,128)(2,1)} copy(bf16[2,256,1024]{2,1,0:T(8,128)(2,1)} %shard_map.73) | data formatting | bytes 2097152
  (9 shorter events, 0.1 us)
Async XLA Ops:
  0.0 0.7 copy-start

commit v3 on v2

--- a/solution.py
+++ b/solution.py
@@ -111,9 +111,12 @@
     for s in range(2):
         for k in ("yp", "ym", "xh", "fa", "fb", "pyp", "pym", "x2"):
             T[k, s] = links.ticket()
-
-    def own(s):
-        links.start(T["xh", s], source.at[s], slot(0, 0, s), "xh")
+    T["pfa"], T["pfb"] = links.ticket(), links.ticket()
+
+    def own(s, first):
+        if not first:
+            links.start(T["xh", s], source.at[s], slot(0, 0, s), "xh")
+            return
         links.start(T["yp", s], source.at[s], slot(0, 0, s), "yp")
         links.start(T["ym", s], source.at[s], slot(0, 0, s), "ym")
 
@@ -131,14 +134,23 @@
     def across(s):
         links.arrive(T["fa", s], slot(0, 2, s, low), "ym")
         links.arrive(T["fb", s], slot(0, 2, s, high), "yp")
-        links.start(T["x2", s], slot(0, 2, s), slot(0, 2, s), "xh")
+        if s == 0:
+            links.start(T["x2", s], slot(0, 2, s), slot(0, 2, s), "xh")
 
     def sides(s):
         links.arrive(T["pyp", s], slot(1, 3, s), "ym")
+        if s == 1:
+            links.start(T["pfa"], slot(1, 3, s, low), slot(1, 3, s, low), "yp")
         links.arrive(T["pym", s], slot(1, 1, s), "yp")
+        if s == 1:
+            links.start(T["pfb"], slot(1, 1, s, high), slot(1, 1, s, high), "ym")
 
     def last(s):
-        links.arrive(T["x2", s], slot(1, 2, s), "xh")
+        if s == 0:
+            links.arrive(T["x2", s], slot(1, 2, s), "xh")
+        else:
+            links.arrive(T["pfa"], slot(1, 2, s, low), "ym")
+            links.arrive(T["pfb"], slot(1, 2, s, high), "yp")
 
     return dict(own=own, forward=forward, partner=partner, across=across, sides=sides, last=last, shard=shard)
 
@@ -172,7 +184,7 @@
     return xl * 8 + z * 2 + core
 
 
-def column_flow(links, buf, place=by_rank):
+def column_flow(links, buf, place=by_rank, far_by_x=False):
     ctx = lax.axis_index("ctx")
     z, xl, core = ctx // 4, (ctx // 2) % 2, ctx % 2
     rows = buf.shape[1]
@@ -184,7 +196,7 @@
         return ref if part is None else ref.at[pl.ds(part * half, half)]
 
     T = {}
-    for k in ("zp", "zm", "xl0", "xl1", "fa", "fb", "pzp0", "pzp1", "pzm0", "pzm1", "pfa", "pfb"):
+    for k in ("zp", "zm", "xl0", "xl1", "fa", "fb", "pzp0", "pzp1", "pzm0", "pzm1", "pfa", "pfb", "x2"):
         T[k] = links.ticket()
     for dx in range(2):
         for dz in range(4):
@@ -219,9 +231,18 @@
     def across():
         links.arrive(T["fa"], slot(0, 2, 0, 0), "zm")
         links.arrive(T["fb"], slot(0, 2, 0, 1), "zp")
+        if far_by_x:
+            links.start(T["x2"], slot(0, 2), slot(0, 2), "xl")
         share(0, 2)
 
     def sides():
+        if far_by_x:
+            for part in range(2):
+                links.arrive(T[f"pzp{part}"], slot(1, 3, 0, part), "zm")
+                links.arrive(T[f"pzm{part}"], slot(1, 1, 0, part), "zp")
+            share(1, 3)
+            share(1, 1)
+            return
         links.arrive(T["pzp0"], slot(1, 3, 0, 0), "zm")
         links.start(T["pfa"], slot(1, 3, 0, 0), slot(1, 3, 0, 0), "zp")
         links.arrive(T["pzm0"], slot(1, 1, 0, 0), "zp")
@@ -232,6 +253,10 @@
         share(1, 1)
 
     def last():
+        if far_by_x:
+            links.arrive(T["x2"], slot(1, 2), "xl")
+            share(1, 2)
+            return
         links.arrive(T["pfa"], slot(1, 2, 0, 0), "zm")
         links.arrive(T["pfb"], slot(1, 2, 0, 1), "zp")
         share(1, 2)
@@ -245,16 +270,16 @@
                 last=last, shared=shared, everything=everything)
 
 
-def attend(first_pair, pair, q_buf, kv_buf, query_pos, key_pos, peaks, sums, out):
+def attend(s, first_pair, pair, q_buf, kv_buf, query_pos, key_pos, peaks, sums, out):
     rows = q_buf.shape[1]
     heads = out.shape[2] // HEAD_DIM
     scale = math.log2(math.e) / math.sqrt(HEAD_DIM)
 
-    def body(i, _):
-        s, h = i // heads, i % heads
-        at = pl.multiple_of(s * rows, rows)
-        keys = kv_buf[pl.ds(pair * 8, 8), pl.ds(at, rows), :].reshape(8 * rows, HEAD_DIM)
-        values = kv_buf[pl.ds(pair * 8, 8), pl.ds(2 * rows + at, rows), :].reshape(8 * rows, HEAD_DIM)
+    def body(h, _):
+        i = s * heads + h
+        held = pl.ds(s * 16 + pair * 8, 8)
+        keys = kv_buf[held, :rows, :].reshape(8 * rows, HEAD_DIM)
+        values = kv_buf[held, rows:, :].reshape(8 * rows, HEAD_DIM)
         scores = lax.dot_general(
             q_buf[i], keys, (((1,), (1,)), ((), ())), preferred_element_type=jnp.float32
         )
@@ -262,21 +287,21 @@
         scores = jnp.where(allowed, scores, masked_score)
         peak = jnp.maximum(jnp.max(scores, axis=1, keepdims=True), 1e-10 * masked_score)
         if not first_pair:
-            before = peaks[i, :, :1]
+            before = peaks[h, :, :1]
             peak = jnp.maximum(peak, before)
         weights = jnp.exp2((scores - peak) * scale).astype(jnp.bfloat16)
         both = jnp.concatenate([values, jnp.ones_like(values)], axis=1)
         summed = jnp.dot(weights, both, preferred_element_type=jnp.float32)
         if first_pair:
-            peaks[i] = jnp.broadcast_to(peak, peaks.shape[1:])
-            sums[i] = summed
+            peaks[h] = jnp.broadcast_to(peak, peaks.shape[1:])
+            sums[h] = summed
         else:
-            summed = summed + sums[i] * jnp.exp2((before - peak) * scale)
+            summed = summed + sums[h] * jnp.exp2((before - peak) * scale)
             mean = summed[:, :HEAD_DIM] / summed[:, HEAD_DIM:]
             out[s, :, pl.ds(pl.multiple_of(h * HEAD_DIM, HEAD_DIM), HEAD_DIM)] = mean.astype(jnp.bfloat16)
         return 0
 
-    lax.fori_loop(0, 2 * heads, body, 0)
+    lax.fori_loop(0, heads, body, 0)
 
 
 def mix_kernel(tokens, wq, wk, wv, wo, gain, cosine, sine, query_pos, key_pos, mixed,
@@ -290,47 +315,66 @@
     width = qw + 2 * kw
     heads = qw // HEAD_DIM
     mine = [
+        pltpu.make_async_copy(tokens, tbuf.at[pl.ds(tp * 2, 2)], local.at[3]),
         pltpu.make_async_copy(wq, wbuf.at[ctx, :, pl.ds(0, qw)], local.at[0]),
         pltpu.make_async_copy(wk, wbuf.at[ctx, :, pl.ds(qw, kw)], local.at[1]),
         pltpu.make_async_copy(wv, wbuf.at[ctx, :, pl.ds(qw + kw, kw)], local.at[2]),
-        pltpu.make_async_copy(tokens, tbuf.at[pl.ds(tp * 2, 2)], local.at[3]),
         pltpu.make_async_copy(wo, wobuf.at[ctx], local.at[4]),
     ]
-    for c in (mine[3], *mine[:3], mine[4]):
+    for c in mine:
         c.start()
     t = token_flow(links, tbuf, tokens)
     w = column_flow(links, wbuf)
     statistics = squares_flow(links, squares)
-    o = column_flow(links, wobuf)
-    kv = column_flow(links, kvbuf, by_pair)
-    mine[3].wait()
+    o = column_flow(links, wobuf, far_by_x=True)
+    kv = [
+        column_flow(links, kvbuf, lambda z_, xl_, core_, s=s: s * 16 + by_pair(z_, xl_, core_), far_by_x=True)
+        for s in range(2)
+    ]
+    links.greet(("yp", "ym", "y2", "xh", "xhyp", "xhym", "xhy2", "zp", "zm", "xl", "co"))
+    t["own"](0, first=True)
+    for c in mine[1:4]:
+        c.wait()
+    w["own_x"](0)
+    w["own_z"]()
+    t["own"](1, first=False)
+    w["own_x"](1)
+    t["own"](1, first=True)
+    t["own"](0, first=False)
+    mine[0].wait()
     for s in range(2):
         wide = tbuf[tp * 2 + s].astype(jnp.float32)
         squares[tp, s] = lax.dot_general(
             jnp.ones((8, wide.shape[1]), jnp.float32), wide * wide, (((1,), (1,)), ((), ())),
             precision=lax.Precision.HIGHEST, preferred_element_type=jnp.float32,
         )
-    for c in mine[:3]:
-        c.wait()
-    links.greet(("yp", "ym", "y2", "xh", "xhyp", "xhym", "xhy2", "zp", "zm", "xl", "co"))
     statistics["own"]()
-    w["own_x"](0)
-    t["own"](0)
-    w["own_z"]()
-    w["own_x"](1)
-    t["own"](1)
     acc[...] = jnp.zeros_like(acc)
     mine[4].wait()
 
+    def multiply(shard):
+        wide = tbuf[pl.ds(shard * 2, 2)].astype(jnp.float32).reshape(2 * rows, tokens.shape[2])
+        x = (wide * factors[:, :1] * gain[shard]).astype(jnp.bfloat16)
+        weights = wbuf[pl.ds(2 * shard, 2)].reshape(x.shape[1], width)
+        acc[...] += jnp.dot(x, weights, preferred_element_type=jnp.float32)
+
+    def run(dx, first, count, stride=1):
+        def body(i, _):
+            multiply((tp // 4 + dx) % 2 * 4 + (tp % 4 + first + stride * i) % 4)
+            return 0
+
+        lax.fori_loop(0, count, body, 0)
+
+    own_column, other_column = [[(dx, dz) for dz in range(4)] for dx in range(2)]
+    near = (xl + tp % 4) % 2
     t["forward"](0)
+    w["partner"](0)
     w["forward"]()
-    w["partner"](0)
-    t["partner"](0)
     t["forward"](1)
+    t["partner"](1)
+    w["across"]()
     w["partner"](1)
-    w["across"]()
     t["across"](0)
-    t["partner"](1)
     t["across"](1)
     o["own_x"](0)
     o["own_x"](1)
@@ -341,37 +385,23 @@
         for i in range(1, 8):
             total = total + squares[i, s]
         factor = lax.rsqrt(total[:1] * (1.0 / features) + norm_eps)
-        factors[s] = jnp.transpose(jnp.broadcast_to(factor, (128, rows)))
+        factors[s * rows:(s + 1) * rows] = jnp.transpose(jnp.broadcast_to(factor, (128, rows)))
+    w["shared"](own_column)
+    t["partner"](0)
+    run(0, near, 2, 2)
     w["sides"]()
     o["own_z"]()
+    t["sides"](1)
+    w["last"]()
+    w["shared"](other_column)
+    run(0, 1 - near, 2, 2)
+    run(1, 0, 1)
     t["sides"](0)
-    w["last"]()
-    w["shared"](w["everything"])
-
-    def multiply(j, s):
-        dx, dy = j // 4, j % 4
-        shard = (tp // 4 + dx) % 2 * 4 + (tp % 4 + dy) % 4
-        wide = tbuf[shard * 2 + s].astype(jnp.float32)
-        x = (wide * factors[s, :, :1] * gain[shard]).astype(jnp.bfloat16)
-        weights = wbuf[pl.ds(2 * shard, 2)].reshape(x.shape[1], width)
-        acc[s] += jnp.dot(x, weights, preferred_element_type=jnp.float32)
-
-    def run(first, count):
-        def body(i, _):
-            multiply(first + i // 2, i % 2)
-            return 0
-
-        lax.fori_loop(0, 2 * count, body, 0)
-
-    run(0, 5)
-    o["forward"]()
-    t["sides"](1)
-    run(5, 1)
-    run(7, 1)
-    o["across"]()
+    run(1, 1, 2, 2)
     t["last"](0)
     t["last"](1)
-    run(6, 1)
+    o["forward"]()
+    run(1, 2, 1)
 
     own = by_pair(z, xl, core)
 
@@ -379,90 +409,117 @@
         return x * cosine[s] + pltpu.roll(x, HEAD_DIM // 2, 1) * sine[s]
 
     for s in range(2):
-        kvbuf[own, s * rows:(s + 1) * rows] = turn(acc[s, :, qw:qw + kw], s).astype(jnp.bfloat16)
-        kvbuf[own, (2 + s) * rows:(3 + s) * rows] = acc[s, :, qw + kw:].astype(jnp.bfloat16)
-    kv["own_x"](0)
-    kv["own_z"]()
-    kv["own_x"](1)
+        at = pl.ds(s * rows, rows)
+        kvbuf[s * 16 + own, :rows] = turn(acc[at, qw:qw + kw], s).astype(jnp.bfloat16)
+        kvbuf[s * 16 + own, rows:] = acc[at, qw + kw:].astype(jnp.bfloat16)
+    for s in range(2):
+        kv[s]["own_x"](0)
+        kv[s]["own_z"]()
+        kv[s]["own_x"](1)
     for s in range(2):
         for h in range(heads):
-            qbuf[s * heads + h] = turn(acc[s, :, h * HEAD_DIM:(h + 1) * HEAD_DIM], s).astype(jnp.bfloat16)
-    kv["partner"](0)
-    kv["forward"]()
-    kv["partner"](1)
-    kv["across"]()
-    kv["shared"]([(0, dz) for dz in range(4)])
-    kv["sides"]()
+            qbuf[s * heads + h] = turn(acc[pl.ds(s * rows, rows), h * HEAD_DIM:(h + 1) * HEAD_DIM], s).astype(jnp.bfloat16)
+
+    def look(s, first_pair):
+        attend(s, first_pair, xl if first_pair else 1 - xl, qbuf, kvbuf, query_pos, key_pos, peaks, sums, attended)
+
+    half = mixed.shape[2] // 2
+    cut = [pl.ds(0, half), pl.ds(half, half)]
+
+    def term(dx, dy, s):
+        return (dx * 4 + dy) * 2 + s
+
+    def products(s, first, count):
+        def body(i, _):
+            rel = first + i
+            block = (tp // 4 + rel // 4) % 2 * 4 + (tp % 4 + rel % 4) % 4
+            for c in range(2):
+                terms[rel * 2 + s, :, c * half:(c + 1) * half] = jnp.dot(
+                    attended[s], wobuf[2 * block + c], preferred_element_type=jnp.float32
+                ).astype(jnp.bfloat16)
+            return 0
+
+        lax.fori_loop(0, count, body, 0)
+
+    R = {(k, s): links.ticket() for s in range(2) for k in ("x", "yp", "ym", "h0", "h1", "zyp0", "zyp1", "zym0", "zym1", "zx")}
+
+    def wide(ref):
+        return ref[...].astype(jnp.float32)
+
+    def open_sums(s):
+        products(s, 6, 1)
+        links.start(R["x", s], terms.at[term(1, 2, s)], from_x.at[s], "xh")
+        products(s, 5, 1)
+        links.start(R["yp", s], terms.at[term(1, 1, s)], from_y.at[s], "yp")
+        products(s, 7, 1)
+        links.start(R["ym", s], terms.at[term(1, 3, s)], from_y.at[2 + s], "ym")
+        products(s, 0, 5)
+
+    def far(s):
+        links.arrive(R["x", s], from_x.at[s])
+        here = terms.at[term(0, 2, s)]
+        here[...] = (wide(here) + wide(from_x.at[s])).astype(jnp.bfloat16)
+        for c, to in ((0, "yp"), (1, "ym")):
+            links.start(R[f"h{c}", s], here.at[:, cut[c]], halves.at[2 * c + s], to)
+        links.start(R["zyp1", s], terms.at[term(0, 1, s), :, cut[1]], last_y.at[s, :, cut[1]], "yp")
+        links.start(R["zym0", s], terms.at[term(0, 3, s), :, cut[0]], last_y.at[2 + s, :, cut[0]], "ym")
+
+    def over(s):
+        links.arrive(R["yp", s], from_y.at[s])
+        links.arrive(R["ym", s], from_y.at[2 + s])
+        here = terms.at[term(1, 0, s)]
+        here[...] = (wide(here) + wide(from_y.at[s]) + wide(from_y.at[2 + s])).astype(jnp.bfloat16)
+        links.start(R["zx", s], here, last_x.at[s], "xh")
+
+    def close(s):
+        for c, dy, k, to in ((0, 1, "zyp0", "yp"), (1, 3, "zym1", "ym")):
+            links.arrive(R[f"h{c}", s], halves.at[2 * c + s])
+            here = terms.at[term(0, dy, s), :, cut[c]]
+            here[...] = (wide(here) + wide(halves.at[2 * c + s])).astype(jnp.bfloat16)
+            links.start(R[k, s], here, last_y.at[2 * c + s, :, cut[c]], to)
+
+    def result(s):
+        links.arrive(R["zx", s], last_x.at[s])
+        for c in range(2):
+            links.arrive(R[f"zyp{c}", s], last_y.at[s, :, cut[c]])
+            links.arrive(R[f"zym{c}", s], last_y.at[2 + s, :, cut[c]])
+        total = wide(terms.at[term(0, 0, s)]) + wide(last_x.at[s]) + wide(last_y.at[s]) + wide(last_y.at[2 + s])
+        mixed[s] = total.astype(jnp.bfloat16)
+
+    for s in range(2):
+        kv[s]["partner"](0)
+        kv[s]["forward"]()
+        kv[s]["partner"](1)
     o["partner"](0)
     o["partner"](1)
-    attend(True, xl, qbuf, kvbuf, query_pos, key_pos, peaks, sums, attended)
-    kv["last"]()
-    kv["shared"]([(1, dz) for dz in range(4)])
+    for s in range(2):
+        kv[s]["across"]()
+    o["across"]()
+    kv[0]["shared"](own_column)
+    look(0, True)
+    kv[0]["sides"]()
+    kv[1]["sides"]()
+    kv[0]["last"]()
+    kv[1]["last"]()
+    kv[0]["shared"](other_column)
+    look(0, False)
     o["sides"]()
-    attend(False, 1 - xl, qbuf, kvbuf, query_pos, key_pos, peaks, sums, attended)
     o["last"]()
-    o["shared"](o["everything"])
-
-    half = terms.shape[2]
-
-    def term(dx, dy, c):
-        return (dx * 4 + dy) * 2 + c
-
-    def products(first, count):
-        def body(i, _):
-            rel, c = first + i // 2, i % 2
-            block = (tp // 4 + rel // 4) % 2 * 4 + (tp % 4 + rel % 4) % 4
-            terms[2 * first + i] = jnp.dot(
-                attended[...].reshape(2 * rows, qw), wobuf[2 * block + c], preferred_element_type=jnp.float32
-            ).astype(jnp.bfloat16)
-            return 0
-
-        lax.fori_loop(0, 2 * count, body, 0)
-
-    R = {}
-    for k in ("x", "yp", "ym", "h", "zyp", "zym", "zx"):
-        for c in range(2):
-            R[k, c] = links.ticket()
-
-    def add(index, *others):
-        total = terms[index].astype(jnp.float32)
-        for ref in others:
-            total = total + ref[...].astype(jnp.float32)
-        return total
-
-    products(6, 1)
-    for c in range(2):
-        links.start(R["x", c], terms.at[term(1, 2, c)], from_x.at[c], "xh")
-    products(5, 1)
-    for c in range(2):
-        links.start(R["yp", c], terms.at[term(1, 1, c)], from_y.at[c], "yp")
-    products(7, 1)
-    for c in range(2):
-        links.start(R["ym", c], terms.at[term(1, 3, c)], from_y.at[2 + c], "ym")
-    products(0, 5)
-    for c, to in ((0, "yp"), (1, "ym")):
-        links.arrive(R["x", c], from_x.at[c])
-        terms[term(0, 2, c)] = add(term(0, 2, c), from_x.at[c]).astype(jnp.bfloat16)
-        links.start(R["h", c], terms.at[term(0, 2, c)], halves.at[c], to)
-    links.start(R["zyp", 1], terms.at[term(0, 1, 1)], last_y.at[1], "yp")
-    links.start(R["zym", 0], terms.at[term(0, 3, 0)], last_y.at[2], "ym")
-    for c in range(2):
-        links.arrive(R["yp", c], from_y.at[c])
-        links.arrive(R["ym", c], from_y.at[2 + c])
-        terms[term(1, 0, c)] = add(term(1, 0, c), from_y.at[c], from_y.at[2 + c]).astype(jnp.bfloat16)
-        links.start(R["zx", c], terms.at[term(1, 0, c)], last_x.at[c], "xh")
-    links.arrive(R["h", 0], halves.at[0])
-    terms[term(0, 1, 0)] = add(term(0, 1, 0), halves.at[0]).astype(jnp.bfloat16)
-    links.start(R["zyp", 0], terms.at[term(0, 1, 0)], last_y.at[0], "yp")
-    links.arrive(R["h", 1], halves.at[1])
-    terms[term(0, 3, 1)] = add(term(0, 3, 1), halves.at[1]).astype(jnp.bfloat16)
-    links.start(R["zym", 1], terms.at[term(0, 3, 1)], last_y.at[3], "ym")
-    for c in range(2):
-        links.arrive(R["zx", c], last_x.at[c])
-        links.arrive(R["zyp", c], last_y.at[c])
-        links.arrive(R["zym", c], last_y.at[2 + c])
-        total = add(term(0, 0, c), last_x.at[c], last_y.at[c], last_y.at[2 + c])
-        mixed[:, :, c * half:(c + 1) * half] = total.astype(jnp.bfloat16).reshape(2, rows, half)
+    o["shared"](own_column + other_column)
+    open_sums(0)
+    kv[1]["shared"](own_column)
+    look(1, True)
+    far(0)
+    over(0)
+    kv[1]["shared"](other_column)
+    look(1, False)
+    open_sums(1)
+    close(0)
+    far(1)
+    over(1)
+    close(1)
+    result(0)
+    result(1)
     links.finish()
 
 
@@ -482,7 +539,6 @@
     query_pos = jnp.broadcast_to(query_pos[:, :, None], (seqs, rows, 128))
     anyspace = pl.BlockSpec(memory_space=pl.ANY)
     vmem = pl.BlockSpec(memory_space=pltpu.VMEM)
-    half = depth // 2
     return pl.pallas_call(
         mix_kernel,
         out_shape=jax.ShapeDtypeStruct(tokens.shape, bf16),
@@ -491,23 +547,23 @@
         scratch_shapes=[
             pltpu.VMEM((n_tp * seqs, rows, depth), bf16),
             pltpu.VMEM((n_ctx, w_query.shape[0], width), bf16),
-            pltpu.VMEM((seqs, rows, width), f32),
+            pltpu.VMEM((seqs * rows, width), f32),
             pltpu.VMEM((n_tp, seqs, 8, rows), f32),
-            pltpu.VMEM((seqs, rows, 128), f32),
+            pltpu.VMEM((seqs * rows, 128), f32),
             pltpu.VMEM((n_ctx, *w_out.shape), bf16),
-            pltpu.VMEM((n_ctx, 2 * seqs * rows, HEAD_DIM), bf16),
+            pltpu.VMEM((seqs * n_ctx, 2 * rows, HEAD_DIM), bf16),
             pltpu.VMEM((seqs * heads, rows, HEAD_DIM), bf16),
-            pltpu.VMEM((seqs * heads, rows, 128), f32),
-            pltpu.VMEM((seqs * heads, rows, 2 * HEAD_DIM), f32),
+            pltpu.VMEM((heads, rows, 128), f32),
+            pltpu.VMEM((heads, rows, 2 * HEAD_DIM), f32),
             pltpu.VMEM((seqs, rows, qw), bf16),
-            pltpu.VMEM((2 * n_tp, seqs * rows, half), bf16),
-            pltpu.VMEM((2, seqs * rows, half), bf16),
-            pltpu.VMEM((4, seqs * rows, half), bf16),
-            pltpu.VMEM((2, seqs * rows, half), bf16),
-            pltpu.VMEM((4, seqs * rows, half), bf16),
-            pltpu.VMEM((2, seqs * rows, half), bf16),
-            pltpu.SemaphoreType.DMA((104,)),
-            pltpu.SemaphoreType.DMA((104,)),
+            pltpu.VMEM((n_tp * seqs, rows, depth), bf16),
+            pltpu.VMEM((seqs, rows, depth), bf16),
+            pltpu.VMEM((2 * seqs, rows, depth), bf16),
+            pltpu.VMEM((2 * seqs, rows, depth // 2), bf16),
+            pltpu.VMEM((2 * seqs, rows, depth), bf16),
+            pltpu.VMEM((seqs, rows, depth), bf16),
+            pltpu.SemaphoreType.DMA((144,)),
+            pltpu.SemaphoreType.DMA((144,)),
             pltpu.SemaphoreType.DMA((5,)),
         ],
         compiler_params=pltpu.CompilerParams(

time: 208 us -> 183 us (0.88)
  Pallas kernels: 200 us -> 176 us
    pallas_call x1, Pallas kernels: 200 us -> 176 us  [per_device(): pl.pallas_call(mix_kernel, out_shape=jax.ShapeDtypeStruct(tokens.shape, b...]
where the time goes in v3:
time: 183 us
  Pallas kernels  176 us (96%)
  local copies, waits for them, and re-layouts  4.72 us (3%)
  other arithmetic  2.02 us (1%)
    pallas_call x1, Pallas kernels, per_device(): pl.pallas_call(mix_kernel, out_shape=jax.ShapeDtypeStruct(tokens.shape, b...  176 us

profile of v3, /device:TPU:0, one launch (start us, length us, event | category | flops | bytes accessed | tf_op | source)
XLA Modules:
  0.0 183.3 jit_solution(17408248128377564465)
XLA Ops:
  0.0 0.0 copy-start
  0.0 0.7 copy-done
  0.7 0.1 dynamic-slice
  0.8 0.1 broadcast_bitcast_fusion
  0.9 0.1 add.34
  1.0 0.7 reshape.24.key_pos
  1.7 0.9 broadcast_in_dim.2.query_pos
  2.5 1.0 fusion
  3.5 1.0 pad_maximum_fusion
  4.5 176.5 %shard_map.73 = bf16[2,256,1024]{2,1,0:T(8,128)(2,1)} custom-call(bf16[2,256,1024]{2,1,0:T(8,128)(2,1)} %tokens.1, bf16[512,512]{1,0:T(8,128)(2,1)} %wq.1, bf16[512,128]{1,0:T(8,128)(2,1)} %wk.1, bf16[512,128]{1,0:T(8,128)(2,1)} %wv.1, bf16[512,512]{1,0:T(8,128)(2,1)} %wo.1, f32[8,1,1024]{2,1,0:T(1,128)} %bitcast.13, ...), custom_call_target="tpu_custom_call" | custom-call | tf_op jit(solution)/shard_map/pallas_call | solution.py:542
  181.0 2.3 %copy.13 = bf16[2,256,1024]{2,1,0:T(8,128)(2,1)} copy(bf16[2,256,1024]{2,1,0:T(8,128)(2,1)} %shard_map.73) | data formatting | bytes 2097152
  (9 shorter events, 0.1 us)
Async XLA Ops:
  0.0 0.7 copy-start

commit v4 on v3

--- a/solution.py
+++ b/solution.py
@@ -22,14 +22,6 @@
         ends.append(at)
     both = jnp.concatenate(arrays, axis=along)
     return tuple(jnp.split(lax.all_gather(both, axis, axis=dim, tiled=True), ends, axis=along))
-
-
-def angles(token_position):
-    half = HEAD_DIM // 2
-    freqs = jnp.exp(-(2.0 * jnp.arange(half, dtype=jnp.float32) / HEAD_DIM) * math.log(theta_base))
-    angle = token_position.astype(jnp.float32)[..., None] * freqs
-    cosine, sine = jnp.cos(angle), jnp.sin(angle)
-    return jnp.concatenate([cosine, cosine], axis=-1), jnp.concatenate([-sine, sine], axis=-1)
 
 
 MESH = pl.DeviceIdType.MESH
@@ -304,8 +296,8 @@
     lax.fori_loop(0, heads, body, 0)
 
 
-def mix_kernel(tokens, wq, wk, wv, wo, gain, cosine, sine, query_pos, key_pos, mixed,
-               tbuf, wbuf, acc, squares, factors, wobuf, kvbuf, qbuf, peaks, sums, attended,
+def mix_kernel(tokens, wq, wk, wv, wo, span_order, gain, freqs, mixed,
+               cosine, sine, query_pos, key_pos, tbuf, wbuf, acc, squares, factors, wobuf, kvbuf, qbuf, peaks, sums, attended,
                terms, from_x, from_y, halves, last_y, last_x, send, recv, local):
     links = Links(send, recv)
     ctx, tp = lax.axis_index("ctx"), lax.axis_index("tp")
@@ -365,6 +357,24 @@
 
         lax.fori_loop(0, count, body, 0)
 
+    block_rows = 16 * rows // span_order.shape[1]
+    per_rank = rows // block_rows
+    lane = lax.broadcasted_iota(jnp.int32, (1, block_rows), 1)
+    down = lax.broadcasted_iota(jnp.int32, (block_rows, HEAD_DIM), 0)
+    sign = jnp.where(lax.broadcasted_iota(jnp.int32, (1, HEAD_DIM), 1) < HEAD_DIM // 2, -1.0, 1.0)
+    for s in range(2):
+        for i in range(16 * per_rank):
+            rank, part = i // per_rank, i % per_rank
+            at = ((rank // 4 * 2 + rank % 2) * per_rank + part) * block_rows
+            key_pos[s * 2 + rank // 2 % 2, :, at:at + block_rows] = span_order[s, i] * block_rows + lane
+        for part in range(per_rank):
+            at = slice(part * block_rows, (part + 1) * block_rows)
+            position = span_order[s, ctx * per_rank + part] * block_rows + down
+            query_pos[s, at] = position
+            angle = position.astype(jnp.float32) * freqs[...]
+            cosine[s, at] = jnp.cos(angle)
+            sine[s, at] = jnp.sin(angle) * sign
+
     own_column, other_column = [[(dx, dz) for dz in range(4)] for dx in range(2)]
     near = (xl + tp % 4) % 2
     t["forward"](0)
@@ -529,22 +539,22 @@
     qw = w_query.shape[1]
     width = qw + w_key.shape[1] + value_weight.shape[1]
     heads = qw // HEAD_DIM
-    blocks = span_order.shape[1]
-    block_rows = n_ctx * rows // blocks
-    bf16, f32 = jnp.bfloat16, jnp.float32
-    position = (span_order[:, :, None] * block_rows + jnp.arange(block_rows, dtype=jnp.int32)).reshape(seqs, n_ctx * rows)
-    query_pos = lax.dynamic_slice_in_dim(position, lax.axis_index("ctx") * rows, rows, 1)
-    cosine, sine = angles(query_pos)
-    key_pos = position.reshape(seqs, 4, 2, 2 * rows).transpose(0, 2, 1, 3).reshape(2 * seqs, 1, 8 * rows)
-    query_pos = jnp.broadcast_to(query_pos[:, :, None], (seqs, rows, 128))
+    bf16, f32, i32 = jnp.bfloat16, jnp.float32, jnp.int32
+    order = jnp.arange(HEAD_DIM // 2, dtype=f32)
+    freqs = jnp.exp(-(2.0 * order / HEAD_DIM) * math.log(theta_base))
+    freqs = jnp.concatenate([freqs, freqs])[None]
     anyspace = pl.BlockSpec(memory_space=pl.ANY)
     vmem = pl.BlockSpec(memory_space=pltpu.VMEM)
     return pl.pallas_call(
         mix_kernel,
         out_shape=jax.ShapeDtypeStruct(tokens.shape, bf16),
-        in_specs=[anyspace] * 5 + [vmem] * 5,
+        in_specs=[anyspace] * 5 + [pl.BlockSpec(memory_space=pltpu.SMEM)] + [vmem] * 2,
         out_specs=vmem,
         scratch_shapes=[
+            pltpu.VMEM((seqs, rows, HEAD_DIM), f32),
+            pltpu.VMEM((seqs, rows, HEAD_DIM), f32),
+            pltpu.VMEM((seqs, rows, 128), i32),
+            pltpu.VMEM((2 * seqs, 1, 8 * rows), i32),
             pltpu.VMEM((n_tp * seqs, rows, depth), bf16),
             pltpu.VMEM((n_ctx, w_query.shape[0], width), bf16),
             pltpu.VMEM((seqs * rows, width), f32),
@@ -569,7 +579,7 @@
         compiler_params=pltpu.CompilerParams(
             collective_id=0, has_side_effects=True, vmem_limit_bytes=63 * 2**20
         ),
-    )(tokens, w_query, w_key, value_weight, w_out, norm_gain.reshape(n_tp, 1, depth), cosine, sine, query_pos, key_pos)
+    )(tokens, w_query, w_key, value_weight, w_out, span_order, norm_gain.reshape(n_tp, 1, depth), freqs)
 
 
 def solution(mesh):

time: 183 us -> 179 us (0.978)
  local copies, waits for them, and re-layouts: 4.72 us -> 2.26 us
where the time goes in v4:
time: 179 us
  Pallas kernels  176 us (98%)
  local copies, waits for them, and re-layouts  2.26 us (1%)
    pallas_call x1, Pallas kernels, per_device(): pl.pallas_call(mix_kernel, out_shape=jax.ShapeDtypeStruct(tokens.shape, b...  176 us

profile of v4, /device:TPU:0, one launch (start us, length us, event | category | flops | bytes accessed | tf_op | source)
XLA Modules:
  0.0 179.2 jit_solution(8442432803025179963)
XLA Ops:
  0.0 0.6 maximum_bitcast_fusion.freqs
  0.6 176.3 %shard_map.73 = bf16[2,256,1024]{2,1,0:T(8,128)(2,1)} custom-call(bf16[2,256,1024]{2,1,0:T(8,128)(2,1)} %tokens.1, bf16[512,512]{1,0:T(8,128)(2,1)} %wq.1, bf16[512,128]{1,0:T(8,128)(2,1)} %wk.1, bf16[512,128]{1,0:T(8,128)(2,1)} %wv.1, bf16[512,512]{1,0:T(8,128)(2,1)} %wo.1, s32[2,32]{1,0:T(2,128)} %span_order.1, f32[8,1,1024]{2,1,0:T(1,128)} %bitcast.3, ...), custom_call_target="tpu_custom_call" | custom-call | tf_op jit(solution)/shard_map/pallas_call | solution.py:548
  176.9 2.3 %copy.9 = bf16[2,256,1024]{2,1,0:T(8,128)(2,1)} copy(bf16[2,256,1024]{2,1,0:T(8,128)(2,1)} %shard_map.73) | data formatting | bytes 2097152
  (1 shorter events, 0.0 us)

commit v5 on v4

--- a/solution.py
+++ b/solution.py
@@ -527,8 +527,8 @@
     close(0)
     far(1)
     over(1)
+    result(0)
     close(1)
-    result(0)
     result(1)
     links.finish()
 

time: 179 us -> 179 us (level)
  no operation moved by 1% of the time
where the time goes in v5:
time: 179 us
  Pallas kernels  176 us (98%)
  local copies, waits for them, and re-layouts  2.26 us (1%)
    pallas_call x1, Pallas kernels, per_device(): pl.pallas_call(mix_kernel, out_shape=jax.ShapeDtypeStruct(tokens.shape, b...  176 us

profile of v5, /device:TPU:0, one launch (start us, length us, event | category | flops | bytes accessed | tf_op | source)
XLA Modules:
  0.0 179.2 jit_solution(11828488557075111451)
XLA Ops:
  0.0 0.6 maximum_bitcast_fusion.freqs
  0.6 176.3 %shard_map.73 = bf16[2,256,1024]{2,1,0:T(8,128)(2,1)} custom-call(bf16[2,256,1024]{2,1,0:T(8,128)(2,1)} %tokens.1, bf16[512,512]{1,0:T(8,128)(2,1)} %wq.1, bf16[512,128]{1,0:T(8,128)(2,1)} %wk.1, bf16[512,128]{1,0:T(8,128)(2,1)} %wv.1, bf16[512,512]{1,0:T(8,128)(2,1)} %wo.1, s32[2,32]{1,0:T(2,128)} %span_order.1, f32[8,1,1024]{2,1,0:T(1,128)} %bitcast.3, ...), custom_call_target="tpu_custom_call" | custom-call | tf_op jit(solution)/shard_map/pallas_call | solution.py:548
  176.9 2.3 %copy.9 = bf16[2,256,1024]{2,1,0:T(8,128)(2,1)} copy(bf16[2,256,1024]{2,1,0:T(8,128)(2,1)} %shard_map.73) | data formatting | bytes 2097152
  (1 shorter events, 0.0 us)
